TPU v7x, 64 devices: a 2x2x8 block of a 4x4x8 slice. The times are simulated.
64 devices in a mesh: data: 4 (over x, y), stage: 16 (over z, core).
Axes of the slice: x: 2, y: 2, z: 8, core: 2. Of those that a mesh axis runs over, the one named last changes fastest.
The devices are a block of a 4x4x8 slice.
Arguments:
- x_enc: bfloat16 [256, 512, 2048], P(('data', 'stage')), parts along dimension 0
- enc_len: int32 [256], P(('data', 'stage')), parts along dimension 0
- y: bfloat16 [256, 192, 2048], P(('data', 'stage')), parts along dimension 0
- enc_wqkv: bfloat16 [2, 2048, 3, 16, 128], replicated
- enc_wo: bfloat16 [2, 16, 128, 2048], replicated
- enc_w1: bfloat16 [2, 2048, 6144], replicated
- enc_w2: bfloat16 [2, 6144, 2048], replicated
- dec_wqkv: bfloat16 [2, 2048, 3, 16, 128], replicated
- dec_wo: bfloat16 [2, 16, 128, 2048], replicated
- cross_wq: bfloat16 [2, 2048, 8, 2, 128], replicated
- cross_wkv: bfloat16 [2, 2048, 2, 8, 128], replicated
- cross_wo: bfloat16 [2, 8, 2, 128, 2048], replicated
- dec_w1: bfloat16 [2, 2048, 6144], replicated
- dec_w2: bfloat16 [2, 6144, 2048], replicated
Outputs:
- output: bfloat16 [256, 192, 2048], P(('data', 'stage')), parts along dimension 0
There are 4 independent parts. A program takes and returns all parts, laid end to end along the dimension named above; an argument that names none is the same for every part.
All inputs are finite; a program needn't handle non-finite values.
Results may differ from a plain program's by a relative error of at most 0.0114466.
Values are sent between devices in bfloat16 or wider.
A program may use at most 768 MiB of HBM per device.

v0:
```python
import jax
import jax.numpy as jnp
from jax import lax
from jax.sharding import PartitionSpec as P, NamedSharding


def rms_norm(inputs):
    wide = inputs.astype(jnp.float32)
    return (wide * lax.rsqrt(jnp.mean(wide * wide, axis=-1, keepdims=True) + 1e-6)).astype(jnp.bfloat16)


def attend(query, keys, values, valid):
    scale = query.shape[-1] ** -0.5
    scores = jnp.einsum("bqgrd,bkgd->bgrqk", query, keys, preferred_element_type=jnp.float32) * scale
    attn_probs = jax.nn.softmax(jnp.where(valid, scores, -1e30), axis=-1).astype(jnp.bfloat16)
    return jnp.einsum("bgrqk,bkgd->bqgrd", attn_probs, values, preferred_element_type=jnp.float32).astype(jnp.bfloat16)


def self_block(state, w_qkv, w_out, valid):
    proj_qkv = jnp.einsum("bsd,dthe->tbshe", rms_norm(state), w_qkv, preferred_element_type=jnp.float32).astype(jnp.bfloat16)
    mixed = attend(proj_qkv[0][:, :, :, None, :], proj_qkv[1], proj_qkv[2], valid)
    update = jnp.einsum("bshre,hev->bsv", mixed, w_out, preferred_element_type=jnp.float32)
    return (state.astype(jnp.float32) + update).astype(jnp.bfloat16)


def ffn_block(state, w_in, w_out):
    hidden = jax.nn.gelu(jnp.einsum("bsd,df->bsf", rms_norm(state), w_in, preferred_element_type=jnp.float32)).astype(jnp.bfloat16)
    update = jnp.einsum("bsf,fd->bsd", hidden, w_out, preferred_element_type=jnp.float32)
    return (state.astype(jnp.float32) + update).astype(jnp.bfloat16)


def encoder(x_enc, enc_len, enc_wqkv, enc_wo, enc_w1, enc_w2):
    valid = (jnp.arange(x_enc.shape[1])[None, :] < enc_len[:, None])[:, None, None, None, :]
    state = x_enc
    for layer in range(enc_wqkv.shape[0]):
        state = self_block(state, enc_wqkv[layer], enc_wo[layer], valid)
        state = ffn_block(state, enc_w1[layer], enc_w2[layer])
    return rms_norm(state)


def decoder(y, kv_all, kv_len, dec_wqkv, dec_wo, cross_wq, cross_wo, dec_w1, dec_w2):
    positions = jnp.arange(y.shape[1])
    causal = positions[None, :] <= positions[:, None]
    keep = (jnp.arange(kv_all.shape[3])[None, :] < kv_len[:, None])[:, None, None, None, :]
    state = y
    for layer in range(dec_wqkv.shape[0]):
        state = self_block(state, dec_wqkv[layer], dec_wo[layer], causal)
        query = jnp.einsum("bsd,dgre->bsgre", rms_norm(state), cross_wq[layer], preferred_element_type=jnp.float32).astype(jnp.bfloat16)
        mixed = attend(query, kv_all[layer, 0], kv_all[layer, 1], keep)
        update = jnp.einsum("bsgre,grev->bsv", mixed, cross_wo[layer], preferred_element_type=jnp.float32)
        state = (state.astype(jnp.float32) + update).astype(jnp.bfloat16)
        state = ffn_block(state, dec_w1[layer], dec_w2[layer])
    return state


def solution(mesh):
    stages = mesh.shape["stage"]
    swap = [(source, (source + stages // 2) % stages) for source in range(stages)]
    rows = P(("data", "stage"))
    whole = P()

    def body(x_enc, enc_len, y, enc_wqkv, enc_wo, enc_w1, enc_w2, dec_wqkv, dec_wo, cross_wq, cross_wkv, cross_wo, dec_w1, dec_w2):
        enc_out = encoder(x_enc, enc_len, enc_wqkv, enc_wo, enc_w1, enc_w2)
        kv_all = jnp.einsum("bsd,ldtge->ltbsge", enc_out, cross_wkv, preferred_element_type=jnp.float32).astype(jnp.bfloat16)
        kv_recv = lax.ppermute(kv_all, "stage", swap)
        len_recv = lax.ppermute(enc_len, "stage", swap)
        return decoder(y, kv_recv, len_recv, dec_wqkv, dec_wo, cross_wq, cross_wo, dec_w1, dec_w2)

    return jax.shard_map(body, mesh=mesh, in_specs=(rows, rows, rows) + (whole,) * 11, out_specs=rows, check_vma=False)
```

profile of v0, /device:TPU:28, one launch (start us, length us, event | category | flops | bytes accessed | tf_op | source)
XLA Modules:
  0.0 1727.5 jit_solution(5997637064493649729)
XLA Ops:
  0.7 35.1 %fusion.366 = (bf16[1,2048,3,16,128]{4,3,2,1,0:T(8,128)(2,1)}, bf16[1,2048,3,16,128]{4,3,2,1,0:T(8,128)(2,1)}) fusion(bf16[2,2048,3,16,128]{4,3,2,1,0:T(8,128)(2,1)} %param.17), kind=kLoop, calls=%fused_computation.331 | loop fusion | bytes 100663296 | tf_op jit(solution)/shard_map/slice | solution.py:36
  40.9 62.8 %convert_bitcast_fusion.1 = bf16[3,4,512,16,128]{4,2,3,0,1:T(8,128)(2,1)} fusion(bf16[1,2048,3,16,128]{4,3,2,1,0:T(8,128)(2,1)} %get-tuple-element.8, bf16[4,512,2048]{2,1,0:T(8,128)(2,1)} %param.14, f32[4,512]{1,0:T(4,128)S(1)} %add_rsqrt_fusion.4), kind=kOutput, calls=%fused_computation.100 | convolution fusion | flops 51564773376 | bytes 58728448 | tf_op jit(solution)/shard_map/bsd,dthe->tbshe/dot_general | solution.py:20
  103.8 29.8 %bitcast_reduce_fusion.1 = (f32[4,16,512]{2,1,0:T(8,128)S(1)}, f32[4,16,512,512]{3,2,1,0:T(8,128)}) fusion(pred[4,512]{1,0:T(4,128)(4,1)S(1)} %iota_compare_fusion.2, bf16[3,4,512,16,128]{4,2,3,0,1:T(8,128)(2,1)} %convert_bitcast_fusion.1), kind=kOutput, calls=%fused_computation.9 | convolution fusion | flops 4345266176 | bytes 84019200 | tf_op jit(solution)/shard_map/bqgrd,bkgd->bgrqk/dot_general | solution.py:14
  133.5 21.4 %fusion.4 = f32[4,16,512]{2,1,0:T(8,128)S(1)} fusion(f32[4,16,512,512]{3,2,1,0:T(8,128)} %get-tuple-element.14, f32[4,16,512]{2,1,0:T(8,128)S(1)} %get-tuple-element.13, pred[4,512]{1,0:T(4,128)(4,1)S(1)} %iota_compare_fusion.2), kind=kLoop, calls=%fused_computation.14 | loop fusion | flops 67076096 | bytes 67373056 | tf_op jit(solution)/shard_map/reduce_sum | solution.py:15
  154.9 30.0 %fusion.244.clone.5 = bf16[4,512,16,128]{1,3,2,0:T(8,128)(2,1)} fusion(f32[4,16,512]{2,1,0:T(8,128)S(1)} %fusion.4, f32[4,16,512]{2,1,0:T(8,128)S(1)} %get-tuple-element.13, f32[4,16,512,512]{3,2,1,0:T(8,128)} %get-tuple-element.14, pred[4,512]{1,0:T(4,128)(4,1)S(1)} %iota_compare_fusion.2, ...), kind=kOutput, calls=%fused_computation.204.clone.clone.clone.clone.clone.2 | convolution fusion | flops 4383047680 | bytes 84150272 | tf_op jit(solution)/shard_map/bgrqk,bkgd->bqgrd/dot_general | solution.py:16
  184.9 24.6 %fusion.102 = (f32[4,512]{1,0:T(4,128)S(1)}, bf16[4,512,2048]{2,1,0:T(8,128)(2,1)S(1)}) fusion(bf16[2,16,128,2048]{3,2,1,0:T(8,128)(2,1)} %param.18, bf16[4,512,2048]{2,1,0:T(8,128)(2,1)} %param.14, bf16[4,512,16,128]{1,3,2,0:T(8,128)(2,1)} %fusion.244.clone.5), kind=kOutput, calls=%fused_computation.127 | convolution fusion | flops 17205032960 | bytes 33562624 | tf_op jit(solution)/shard_map/bshre,hev->bsv/dot_general | solution.py:22
  212.8 70.5 %fusion.230.clone.5 = bf16[4,512,6144]{2,1,0:T(8,128)(2,1)} fusion(bf16[2,2048,6144]{2,1,0:T(8,128)(2,1)} %param.19, bf16[4,512,2048]{2,1,0:T(8,128)(2,1)S(1)} %get-tuple-element.16, f32[4,512]{1,0:T(4,128)S(1)} %add_rsqrt_fusion.3), kind=kOutput, calls=%fused_computation.23.clone.clone.clone.clone.clone.clone.2 | convolution fusion | flops 51665436672 | bytes 58728448 | tf_op jit(solution)/shard_map/bsd,df->bsf/dot_general | solution.py:27
  283.4 69.6 %fusion.105 = (f32[4,512]{1,0:T(4,128)S(1)}, bf16[4,512,2048]{2,1,0:T(8,128)(2,1)}) fusion(bf16[2,6144,2048]{2,1,0:T(8,128)(2,1)} %param.20, bf16[4,512,2048]{2,1,0:T(8,128)(2,1)} %copy-done.11, bf16[4,512,6144]{2,1,0:T(8,128)(2,1)} %fusion.230.clone.5), kind=kOutput, calls=%fused_computation.130 | convolution fusion | flops 51564773376 | bytes 67117056 | tf_op jit(solution)/shard_map/bsf,fd->bsd/dot_general | solution.py:28
  353.0 63.0 %convert_bitcast_fusion = bf16[3,4,512,16,128]{4,2,3,0,1:T(8,128)(2,1)} fusion(bf16[1,2048,3,16,128]{4,3,2,1,0:T(8,128)(2,1)} %get-tuple-element.7, bf16[4,512,2048]{2,1,0:T(8,128)(2,1)} %get-tuple-element.18, f32[4,512]{1,0:T(4,128)S(1)} %add_rsqrt_fusion.2), kind=kOutput, calls=%fused_computation.85 | convolution fusion | flops 51564773376 | bytes 58728448 | tf_op jit(solution)/shard_map/bsd,dthe->tbshe/dot_general | solution.py:20
  416.0 29.5 %bitcast_reduce_fusion = (f32[4,16,512]{2,1,0:T(8,128)S(1)}, f32[4,16,512,512]{3,2,1,0:T(8,128)}) fusion(pred[4,512]{1,0:T(4,128)(4,1)S(1)} %copy-done.6, bf16[3,4,512,16,128]{4,2,3,0,1:T(8,128)(2,1)} %convert_bitcast_fusion), kind=kOutput, calls=%fused_computation.5 | convolution fusion | flops 4345266176 | bytes 84019200 | tf_op jit(solution)/shard_map/bqgrd,bkgd->bgrqk/dot_general | solution.py:14
  445.6 21.8 %fusion.5 = f32[4,16,512]{2,1,0:T(8,128)S(1)} fusion(f32[4,16,512,512]{3,2,1,0:T(8,128)} %get-tuple-element.20, f32[4,16,512]{2,1,0:T(8,128)S(1)} %get-tuple-element.19, pred[4,512]{1,0:T(4,128)(4,1)S(1)} %copy-done.6), kind=kLoop, calls=%fused_computation.15 | loop fusion | flops 67076096 | bytes 67373056 | tf_op jit(solution)/shard_map/reduce_sum | solution.py:15
  467.4 29.9 %fusion.250.clone.5 = bf16[4,512,16,128]{1,3,2,0:T(8,128)(2,1)} fusion(f32[4,16,512]{2,1,0:T(8,128)S(1)} %fusion.5, f32[4,16,512]{2,1,0:T(8,128)S(1)} %get-tuple-element.19, f32[4,16,512,512]{3,2,1,0:T(8,128)} %get-tuple-element.20, pred[4,512]{1,0:T(4,128)(4,1)S(1)} %copy-done.6, ...), kind=kOutput, calls=%fused_computation.202.clone.clone.clone.clone.clone.2 | convolution fusion | flops 4383047680 | bytes 84150272 | tf_op jit(solution)/shard_map/bgrqk,bkgd->bqgrd/dot_general | solution.py:16
  497.3 24.3 %fusion.108 = (f32[4,512]{1,0:T(4,128)S(1)}, bf16[4,512,2048]{2,1,0:T(8,128)(2,1)S(1)}) fusion(bf16[2,16,128,2048]{3,2,1,0:T(8,128)(2,1)} %param.18, bf16[4,512,2048]{2,1,0:T(8,128)(2,1)} %get-tuple-element.18, bf16[4,512,16,128]{1,3,2,0:T(8,128)(2,1)} %fusion.250.clone.5), kind=kOutput, calls=%fused_computation.133 | convolution fusion | flops 17205032960 | bytes 33562624 | tf_op jit(solution)/shard_map/bshre,hev->bsv/dot_general | solution.py:22
  524.8 70.7 %fusion.238.clone.5 = bf16[4,512,6144]{2,1,0:T(8,128)(2,1)} fusion(bf16[2,2048,6144]{2,1,0:T(8,128)(2,1)} %param.19, bf16[4,512,2048]{2,1,0:T(8,128)(2,1)S(1)} %get-tuple-element.22, f32[4,512]{1,0:T(4,128)S(1)} %add_rsqrt_fusion.1), kind=kOutput, calls=%fused_computation.31.clone.clone.clone.clone.clone.clone.2 | convolution fusion | flops 51665436672 | bytes 58728448 | tf_op jit(solution)/shard_map/bsd,df->bsf/dot_general | solution.py:27
  595.4 69.7 %fusion.97 = (f32[4,512]{1,0:T(4,128)S(1)}, bf16[4,512,2048]{2,1,0:T(8,128)(2,1)}) fusion(bf16[2,6144,2048]{2,1,0:T(8,128)(2,1)} %param.20, bf16[4,512,2048]{2,1,0:T(8,128)(2,1)} %copy-done.10, bf16[4,512,6144]{2,1,0:T(8,128)(2,1)} %fusion.238.clone.5), kind=kOutput, calls=%fused_computation.122 | convolution fusion | flops 51564773376 | bytes 67117056 | tf_op jit(solution)/shard_map/bsf,fd->bsd/dot_general | solution.py:28
  665.2 44.3 %convert_bitcast_fusion.2 = bf16[2,2,4,512,8,128]{5,3,4,1,0,2:T(8,128)(2,1)} fusion(bf16[2,2048,2,8,128]{4,3,2,1,0:T(8,128)(2,1)} %param.24, bf16[4,512,2048]{2,1,0:T(8,128)(2,1)} %get-tuple-element.24, f32[4,512]{1,0:T(4,128)S(1)} %add_rsqrt_fusion), kind=kOutput, calls=%fused_computation.139 | convolution fusion | flops 34380709888 | bytes 41951232 | tf_op jit(solution)/shard_map/bsd,ldtge->ltbsge/dot_general | solution.py:64
  718.3 35.7 %fusion.365 = (bf16[1,2048,3,16,128]{4,3,2,1,0:T(8,128)(2,1)}, bf16[1,2048,3,16,128]{4,3,2,1,0:T(8,128)(2,1)}) fusion(bf16[2,2048,3,16,128]{4,3,2,1,0:T(8,128)(2,1)} %param.21), kind=kLoop, calls=%fused_computation.330 | loop fusion | bytes 100663296 | tf_op jit(solution)/shard_map/slice | solution.py:47
  754.0 25.8 %convert_bitcast_fusion.4 = bf16[3,4,192,16,128]{4,2,3,0,1:T(8,128)(2,1)} fusion(bf16[1,2048,3,16,128]{4,3,2,1,0:T(8,128)(2,1)} %get-tuple-element.6, bf16[4,192,2048]{2,1,0:T(8,128)(2,1)S(1)} %copy-done.2, f32[4,192]{1,0:T(4,128)S(1)} %add_rsqrt_fusion.10), kind=kOutput, calls=%fused_computation.185 | convolution fusion | flops 19336790016 | bytes 37751808 | tf_op jit(solution)/shard_map/bsd,dthe->tbshe/dot_general | solution.py:20
  793.1 17.0 fusion.202
  824.2 614.1 %collective-permute-done.1 = s32[4]{0:T(128)S(1)} collective-permute-done((s32[4]{0:T(128)S(1)}, s32[4]{0:T(128)S(1)}, u32[]{:S(2)}, u32[]{:S(2)}) %collective-permute-start.1) | collective-permute-done | bytes 48 | tf_op jit(solution)/shard_map/ppermute | solution.py:66
  1438.4 17.8 %fusion.252 = f32[4,8,512,192,2]{2,3,4,1,0:T(8,128)} fusion(bf16[2,2,4,512,8,128]{5,3,4,1,0,2:T(8,128)(2,1)} %collective-permute-done, bf16[2048,8,2,128,1]{3,2,1,0,4:T(2,128)(2,1)} %get-tuple-element.10, bf16[4,192,2048]{2,1,0:T(8,128)(2,1)S(1)} %get-tuple-element.26, f32[4,192]{1,0:T(4,128)S(1)} %add_rsqrt_fusion.9), kind=kOutput, calls=%fused_computation.258 | convolution fusion | flops 8059355136 | bytes 40897536 | tf_op jit(solution)/shard_map/bqgrd,bkgd->bgrqk/dot_general | solution.py:14
  1456.2 27.7 %fusion.381 = (f32[4,8,2,192]{3,2,1,0:T(2,128)S(1)}, f32[4,8,2,192,512]{4,3,2,1,0:T(8,128)}) fusion(f32[4,8,512,192,2]{2,3,4,1,0:T(8,128)} %fusion.252, pred[4,512]{1,0:T(4,128)(4,1)S(1)} %iota_compare_fusion.1), kind=kOutput, calls=%fused_computation.332 | output fusion | flops 37749248 | bytes 50382848 | tf_op jit(solution)/shard_map/sub | solution.py:15
  1483.9 18.2 %fusion.205 = (f32[4,192]{1,0:T(4,128)S(1)}, bf16[4,192,2048]{2,1,0:T(8,128)(2,1)}) fusion(bf16[2,8,2,128,2048]{4,3,2,1,0:T(8,128)(2,1)} %param.25, f32[4,8,2,192,512]{4,3,2,1,0:T(8,128)} %get-tuple-element.28, f32[4,8,2,192]{3,2,1,0:T(2,128)S(1)} %get-tuple-element.27, bf16[2,2,4,512,8,128]{5,3,4,1,0,2:T(8,128)(2,1)} %collective-permute-done, ...), kind=kOutput, calls=%fused_computation.236 | convolution fusion | flops 8076655616 | bytes 44092416 | tf_op jit(solution)/shard_map/bsgre,grev->bsv/dot_general | solution.py:50
  1502.1 27.3 %fusion.266.clone.5 = bf16[4,192,6144]{2,1,0:T(8,128)(2,1)S(1)} fusion(bf16[2,2048,6144]{2,1,0:T(8,128)(2,1)} %param.26, bf16[4,192,2048]{2,1,0:T(8,128)(2,1)} %get-tuple-element.30, f32[4,192]{1,0:T(4,128)S(1)} %add_rsqrt_fusion.8), kind=kOutput, calls=%fused_computation.113.clone.clone.clone.clone.clone.clone.2 | convolution fusion | flops 19374538752 | bytes 37751808 | tf_op jit(solution)/shard_map/bsd,df->bsf/dot_general | solution.py:27
  1529.4 23.8 %fusion.208 = (f32[4,192]{1,0:T(4,128)S(1)}, bf16[4,192,2048]{2,1,0:T(8,128)(2,1)S(1)}) fusion(bf16[2,6144,2048]{2,1,0:T(8,128)(2,1)} %param.27, bf16[4,192,2048]{2,1,0:T(8,128)(2,1)} %get-tuple-element.30, bf16[4,192,6144]{2,1,0:T(8,128)(2,1)S(1)} %fusion.266.clone.5), kind=kOutput, calls=%fused_computation.239 | convolution fusion | flops 19336790016 | bytes 40897536 | tf_op jit(solution)/shard_map/bsf,fd->bsd/dot_general | solution.py:28
  1553.2 26.7 %convert_bitcast_fusion.3 = bf16[3,4,192,16,128]{4,2,3,0,1:T(8,128)(2,1)} fusion(bf16[1,2048,3,16,128]{4,3,2,1,0:T(8,128)(2,1)} %get-tuple-element.5, bf16[4,192,2048]{2,1,0:T(8,128)(2,1)S(1)} %get-tuple-element.32, f32[4,192]{1,0:T(4,128)S(1)} %add_rsqrt_fusion.7), kind=kOutput, calls=%fused_computation.176 | convolution fusion | flops 19336790016 | bytes 37751808 | tf_op jit(solution)/shard_map/bsd,dthe->tbshe/dot_general | solution.py:20
  1593.3 17.0 fusion.211
  1610.3 17.8 %fusion.251 = f32[4,8,512,192,2]{2,3,4,1,0:T(8,128)} fusion(bf16[2,2,4,512,8,128]{5,3,4,1,0,2:T(8,128)(2,1)} %collective-permute-done, bf16[2048,8,2,128,1]{3,2,1,0,4:T(2,128)(2,1)} %get-tuple-element.9, bf16[4,192,2048]{2,1,0:T(8,128)(2,1)S(1)} %get-tuple-element.36, f32[4,192]{1,0:T(4,128)S(1)} %add_rsqrt_fusion.6), kind=kOutput, calls=%fused_computation.255 | convolution fusion | flops 8059355136 | bytes 40897536 | tf_op jit(solution)/shard_map/bqgrd,bkgd->bgrqk/dot_general | solution.py:14
  1628.0 28.2 %fusion.388 = (f32[4,8,2,192]{3,2,1,0:T(2,128)S(1)}, f32[4,8,2,192,512]{4,3,2,1,0:T(8,128)}) fusion(f32[4,8,512,192,2]{2,3,4,1,0:T(8,128)} %fusion.251, pred[4,512]{1,0:T(4,128)(4,1)S(1)} %copy-done.8), kind=kOutput, calls=%fused_computation.333 | output fusion | flops 37749248 | bytes 50382848 | tf_op jit(solution)/shard_map/sub | solution.py:15
  1656.2 18.2 %fusion.214 = (f32[4,192]{1,0:T(4,128)S(1)}, bf16[4,192,2048]{2,1,0:T(8,128)(2,1)}) fusion(bf16[2,8,2,128,2048]{4,3,2,1,0:T(8,128)(2,1)} %param.25, f32[4,8,2,192,512]{4,3,2,1,0:T(8,128)} %get-tuple-element.38, f32[4,8,2,192]{3,2,1,0:T(2,128)S(1)} %get-tuple-element.37, bf16[2,2,4,512,8,128]{5,3,4,1,0,2:T(8,128)(2,1)} %collective-permute-done, ...), kind=kOutput, calls=%fused_computation.245 | convolution fusion | flops 8076655616 | bytes 44092416 | tf_op jit(solution)/shard_map/bsgre,grev->bsv/dot_general | solution.py:50
  1674.4 28.7 %fusion.442 = bf16[4,192,6144]{2,1,0:T(8,128)(2,1)S(1)} fusion(bf16[2,2048,6144]{2,1,0:T(8,128)(2,1)} %param.26, bf16[4,192,2048]{2,1,0:T(8,128)(2,1)} %get-tuple-element.40, f32[4,192]{1,0:T(4,128)S(1)} %add_rsqrt_fusion.5), kind=kOutput, calls=%fused_computation.121.clone.clone.clone.clone.2 | convolution fusion | flops 19374538752 | bytes 37751808 | tf_op jit(solution)/shard_map/bsd,df->bsf/dot_general | solution.py:27
  1703.1 24.0 %fusion.216 = bf16[4,192,2048]{2,1,0:T(8,128)(2,1)} fusion(bf16[4,192,2048]{2,1,0:T(8,128)(2,1)S(1)} %copy-done.13, bf16[2,6144,2048]{2,1,0:T(8,128)(2,1)} %param.27, bf16[4,192,6144]{2,1,0:T(8,128)(2,1)S(1)} %fusion.442), kind=kOutput, calls=%fused_computation.247 | convolution fusion | flops 19332071424 | bytes 40894464 | tf_op jit(solution)/shard_map/bsf,fd->bsd/dot_general | solution.py:28
  (52 shorter events, 62.0 us)
Async XLA Ops:
  0.7 154.2 %copy-start.5 = (pred[4,512]{1,0:T(4,128)(4,1)}, pred[4,512]{1,0:T(4,128)(4,1)S(1)}, u32[]{:S(2)}) copy-start(pred[4,512]{1,0:T(4,128)(4,1)S(1)} %iota_compare_fusion.2) | copy-start | bytes 6148
  209.5 3.3 copy-start.11
  353.0 63.0 %copy-start.6 = (pred[4,512]{1,0:T(4,128)(4,1)S(1)}, pred[4,512]{1,0:T(4,128)(4,1)}, u32[]{:S(2)}) copy-start(pred[4,512]{1,0:T(4,128)(4,1)} %copy-done.5) | copy-start | bytes 6148
  521.6 3.2 copy-start.10
  665.1 52.3 %copy-start.9 = (s32[4]{0:T(128)S(1)}, s32[4]{0:T(128)}, u32[]{:S(2)}) copy-start(s32[4]{0:T(128)} %param.15) | copy-start | bytes 52
  665.1 52.4 %copy-start.2 = (bf16[4,192,2048]{2,1,0:T(8,128)(2,1)S(1)}, bf16[4,192,2048]{2,1,0:T(8,128)(2,1)}, u32[]{:S(2)}) copy-start(bf16[4,192,2048]{2,1,0:T(8,128)(2,1)} %param.16) | copy-start | bytes 9437188
  709.5 728.9 %collective-permute-start = (bf16[2,2,4,512,8,128]{5,3,4,1,0,2:T(8,128)(2,1)}, bf16[2,2,4,512,8,128]{5,3,4,1,0,2:T(8,128)(2,1)}, u32[]{:S(2)}, u32[]{:S(2)}) collective-permute-start(bf16[2,2,4,512,8,128]{5,3,4,1,0,2:T(8,128)(2,1)} %convert_bitcast_fusion.2), channel_id=1, source_target_pairs={{0,8},{1,9},{2,10},{3,11},{4,12},{5,13},{6,14},{7,15},{8,0},{9,1},... | collective-permute-start | bytes 50331656 | tf_op jit(solution)/shard_map/ppermute | solution.py:65
  717.5 720.9 %collective-permute-start.1 = (s32[4]{0:T(128)S(1)}, s32[4]{0:T(128)S(1)}, u32[]{:S(2)}, u32[]{:S(2)}) collective-permute-start(s32[4]{0:T(128)S(1)} %copy-done.9), channel_id=1, source_target_pairs={{0,8},{1,9},{2,10},{3,11},{4,12},{5,13},{6,14},{7,15},{8,0},{9,1},... | collective-permute-start | bytes 56 | tf_op jit(solution)/shard_map/ppermute | solution.py:66
  717.6 75.5 %copy-start.3 = (pred[192,192]{0,1:T(8,128)(4,1)}, pred[192,192]{0,1:T(8,128)(4,1)S(1)}, u32[]{:S(2)}) copy-start(pred[192,192]{0,1:T(8,128)(4,1)S(1)} %iota_compare_fusion) | copy-start | bytes 110596
  784.8 4.6 copy-start.1
  1438.4 17.8 %copy-start.7 = (pred[4,512]{1,0:T(4,128)(4,1)}, pred[4,512]{1,0:T(4,128)(4,1)S(1)}, u32[]{:S(2)}) copy-start(pred[4,512]{1,0:T(4,128)(4,1)S(1)} %iota_compare_fusion.1) | copy-start | bytes 6148
  1553.2 26.7 %copy-start.12 = (bf16[4,192,2048]{2,1,0:T(8,128)(2,1)}, bf16[4,192,2048]{2,1,0:T(8,128)(2,1)S(1)}, u32[]{:S(2)}) copy-start(bf16[4,192,2048]{2,1,0:T(8,128)(2,1)S(1)} %get-tuple-element.32) | copy-start | bytes 9437188
  1553.2 26.7 %copy-start.4 = (pred[192,192]{0,1:T(8,128)(4,1)S(1)}, pred[192,192]{0,1:T(8,128)(4,1)}, u32[]{:S(2)}) copy-start(pred[192,192]{0,1:T(8,128)(4,1)} %copy-done.3) | copy-start | bytes 110596
  1585.0 4.6 copy-start
  1610.3 17.8 %copy-start.8 = (pred[4,512]{1,0:T(4,128)(4,1)S(1)}, pred[4,512]{1,0:T(4,128)(4,1)}, u32[]{:S(2)}) copy-start(pred[4,512]{1,0:T(4,128)(4,1)} %copy-done.7) | copy-start | bytes 6148
  1674.4 28.7 %copy-start.13 = (bf16[4,192,2048]{2,1,0:T(8,128)(2,1)S(1)}, bf16[4,192,2048]{2,1,0:T(8,128)(2,1)}, u32[]{:S(2)}) copy-start(bf16[4,192,2048]{2,1,0:T(8,128)(2,1)} %get-tuple-element.40) | copy-start | bytes 9437188
where the time goes:
time: 1740 us; the launch traced here: 1730 us
  matrix products  891 us (51%)
  waiting for transfers between devices  614 us (35%)
  other arithmetic  113 us (6%)
  local copies, waits for them, and re-layouts  100 us (6%)
    ppermute x1, waiting for transfers between devices, body(): len_recv = lax.ppermute(enc_len, 'stage', swap)  614 us
    dot_general x4, matrix products, ffn_block(): jnp.einsum('bsd,df->bsf', rms_norm(state), w_in, preferred_element_type=j...  197 us
    dot_general x4, matrix products, ffn_block(): jnp.einsum('bsf,fd->bsd', hidden, w_out, preferred_element_type=jnp.float32)  187 us
    dot_general x4, matrix products, self_block(): jnp.einsum('bsd,dthe->tbshe', rms_norm(state), w_qkv, preferred_element_t...  178 us
    dot_general x6, matrix products, attend(): jnp.einsum('bqgrd,bkgd->bgrqk', query, keys, preferred_element_type=jnp.f...  105 us
    dot_general x4, matrix products, self_block(): jnp.einsum('bshre,hev->bsv', mixed, w_out, preferred_element_type=jnp.flo...  82.8 us
    dot_general x2, matrix products, attend(): jnp.einsum('bgrqk,bkgd->bqgrd', attn_probs, values, preferred_element_typ...  59.9 us
    sub x2, other arithmetic, attend(): jax.nn.softmax(jnp.where(valid, scores, -1e+30), axis=-1)  55.8 us
  transfers between devices with their start and end apart: 2, of which 1 were waited for; matrix products, arithmetic and copies ran while one was open for 6% of the time, Pallas kernels for 0%

commit v1 on v0

v1 whole, which is shorter than its diff:
```python
import functools

import jax
import jax.numpy as jnp
from jax import lax
from jax.experimental import pallas as pl
from jax.experimental.pallas import tpu as pltpu
from jax.sharding import PartitionSpec as P

HEAD = 128
LANES = 128
EPS = 1e-6
LOG2E = 1.4426950408889634
F32 = jnp.float32
BF16 = jnp.bfloat16
VMEM_LIMIT = 67043328


def dot(a, b):
    return jnp.dot(a, b, preferred_element_type=F32)


def dot_t(a, b):
    return lax.dot_general(a, b, (((1,), (1,)), ((), ())), preferred_element_type=F32)


def gelu(x):
    k = -2.0 * 0.7978845608028654 * LOG2E
    return x / (1.0 + jnp.exp2(x * (k + (k * 0.044715) * (x * x))))


def softmax_rows(scores, scale):
    top = jnp.max(scores, axis=-1, keepdims=True)
    weight = jnp.exp2((scores - top) * (scale * LOG2E))
    total = jnp.sum(weight, axis=-1, keepdims=True)
    return (weight * (1.0 / total)).astype(BF16)


def attend_units(count, make_scores, scale, finish):
    ahead = make_scores(0)
    for i in range(count):
        now = ahead
        if i + 1 < count:
            ahead = make_scores(i + 1)
        finish(i, softmax_rows(now, scale))


def joined(ref, blocks, rows=slice(None)):
    return jnp.concatenate([ref[c, rows] for c in blocks], axis=1)


def square_sum(ref, first, count):
    total = None
    for c in range(count):
        wide = ref[first + c].astype(F32)
        total = wide * wide if total is None else total + wide * wide
    return total


def settle_norm(sums, rstd, depth):
    mean = jnp.sum(sums[...], axis=-1, keepdims=True) * (1.0 / depth)
    rstd[...] = jnp.broadcast_to(lax.rsqrt(mean + EPS), rstd.shape)
    sums[...] = jnp.zeros_like(sums)


def normalize(state, rstd, dst):
    for c in range(state.shape[0]):
        dst[c] = (state[c].astype(F32) * rstd[...]).astype(BF16)


def add_to_state(state, sums, first, update):
    part = None
    for k in range(update.shape[1] // LANES):
        fresh = (state[first + k].astype(F32) + update[:, k * LANES : (k + 1) * LANES]).astype(BF16)
        state[first + k] = fresh
        wide = fresh.astype(F32)
        part = wide * wide if part is None else part + wide * wide
    sums[...] += part


def put_blocks(dst, first, value, rows=slice(None)):
    for k in range(value.shape[1] // LANES):
        dst[first + k, rows] = value[:, k * LANES : (k + 1) * LANES]


def block_copies(hbm, row0, buf, sems, to_hbm=False):
    blocks, rows = buf.shape[0], buf.shape[1]
    copies = []
    for c in range(blocks):
        there = hbm.at[pl.ds(row0, rows), pl.ds(c * LANES, LANES)]
        here = buf.at[c]
        copies.append(pltpu.make_async_copy(here, there, sems.at[c]) if to_hbm else pltpu.make_async_copy(there, here, sems.at[c]))
    return copies


class Ring:
    def __init__(self, buf, sem):
        self.buf, self.sem = buf, sem

    def copies(self, base, refs):
        return [pltpu.make_async_copy(ref, self.buf.at[base + k], self.sem.at[base + k]) for k, ref in enumerate(refs)]

    def start(self, base, refs):
        for copy in self.copies(base, refs):
            copy.start()

    def wait(self, base, refs):
        for copy in self.copies(base, refs):
            copy.wait()


def at_cols(i, width):
    return pl.ds(pl.multiple_of(i * width, width), width)


def loop(count, step):
    def body(i, carry):
        step(i)
        return carry

    lax.fori_loop(0, count, body, 0)


def load_state(copies, state, sums):
    for c, copy in enumerate(copies):
        copy.wait()
        part = square_sum(state, c, 1)
        if c == 0:
            sums[...] = part
        else:
            sums[...] += part


def ffn_in(xn, big, ring, base, t, tile, piece, row_piece):
    blocks = range(xn.shape[0])
    per = piece // LANES
    for k in range(3):
        for n in range(tile // piece):
            w = ring[base + k, :, n * piece : (n + 1) * piece]
            for m in range(xn.shape[1] // row_piece):
                rows = slice(m * row_piece, (m + 1) * row_piece)
                put_blocks(big, t * (3 * tile // LANES) + (k * tile + n * piece) // LANES, gelu(dot(joined(xn, blocks, rows), w)).astype(BF16), rows)


def ffn_out(state, sums, big, ring, base, t, tile, piece):
    depth_blocks = state.shape[0]
    for n in range(tile // piece):
        total = None
        for k in range(3):
            part = dot(joined(big, range(k * depth_blocks, (k + 1) * depth_blocks)), ring[base + k, :, n * piece : (n + 1) * piece])
            total = part if total is None else total + part
        add_to_state(state, sums, t * (tile // LANES) + n * piece // LANES, total)


def cost(flops, bytes_accessed):
    return pl.CostEstimate(flops=int(flops), bytes_accessed=int(bytes_accessed), transcendentals=0)


def encoder_kernel(first_row, seqs, span, len_ref, x_ref, wqkv, wo, w1, w2, out_ref, h, xn, big, sums, rstd, raw, ring_buf, io_sem, raw_sem, ring_sem):
    layers, depth = wqkv.shape[0], wqkv.shape[1]
    heads = wqkv.shape[3]
    rows = seqs * span
    tile = depth // 2
    tile_heads = tile // HEAD
    piece = min(512, tile)
    row_piece = min(512, rows)
    blocks = depth // LANES
    n_qkv = 6
    scale = HEAD**-0.5

    raws = Ring(raw, raw_sem)
    ring = Ring(ring_buf, ring_sem)

    def qkv_src(layer, j):
        return [wqkv.at[layer, :, j // 2, pl.ds(pl.multiple_of(lax.rem(j, 2) * tile_heads, tile_heads), tile_heads), :]]

    def wo_src(layer):
        return [wo.at[layer, :, pl.ds(n * tile, tile)] for n in range(2)]

    def w1_src(layer, t):
        return [w1.at[layer, :, pl.ds((t * 3 + k) * tile, tile)] for k in range(3)]

    def w2_src(layer, t):
        return [w2.at[layer, pl.ds(k * depth, depth), pl.ds(t * tile, tile)] for k in range(3)]

    load = block_copies(x_ref, first_row, h, io_sem)
    for copy in load:
        copy.start()
    raws.start(0, qkv_src(0, 0))
    load_state(load, h, sums)
    settle_norm(sums, rstd, depth)
    raws.start(1, qkv_src(0, 1))
    ring.start(0, wo_src(0))

    for layer in range(layers):
        last = layer + 1 == layers
        bases = [((5 * layer + g) % 2) * 3 for g in range(6)]

        def qkv_step(j):
            slot = lax.rem(j, 3)
            raws.wait(slot, qkv_src(layer, j))

            @pl.when(j < n_qkv - 2)
            def _():
                raws.start(lax.rem(j + 2, 3), qkv_src(layer, j + 2))

            if not last:

                @pl.when(j >= n_qkv - 2)
                def _():
                    raws.start(lax.rem(j + 2, 3), qkv_src(layer + 1, j + 2 - n_qkv))

            normalize(h, rstd, xn)
            w = raw[slot].reshape(depth, tile)
            for n in range(tile // piece):
                put_blocks(big, j * (tile // LANES) + n * piece // LANES, dot(joined(xn, range(blocks)), w[:, n * piece : (n + 1) * piece]).astype(BF16))

        loop(n_qkv, qkv_step)

        def attend_step(i):
            groups = heads // tile_heads
            b, g = i // groups, lax.rem(i, groups)
            keep = lax.broadcasted_iota(jnp.int32, (1, span), 1) < len_ref[b + first_row // span]
            at = pl.ds(pl.multiple_of(b * span, span), span)

            def head(u, which):
                return which * heads + g * tile_heads + u

            def scores(u):
                return jnp.where(keep, dot_t(big[head(u, 0), at], big[head(u, 1), at]), -1e30 / scale)

            def finish(u, probs):
                xn[head(u, 0), at] = dot(probs, big[head(u, 2), at]).astype(BF16)

            attend_units(tile_heads, scores, scale, finish)

        loop(seqs * (heads // tile_heads), attend_step)

        ring.wait(bases[0], wo_src(layer))
        ring.start(bases[1], w1_src(layer, 0))

        def wo_step(t):
            for n in range(tile // piece):
                add_to_state(h, sums, t * (tile // LANES) + n * piece // LANES, dot(joined(xn, range(blocks)), ring_buf[bases[0] + t, :, n * piece : (n + 1) * piece]))

        loop(2, wo_step)
        settle_norm(sums, rstd, depth)

        def w1_step(t):
            base = jnp.where(t == 0, bases[1], bases[2])
            ring.wait(base, w1_src(layer, 0))

            @pl.when(t == 0)
            def _():
                ring.start(bases[2], w1_src(layer, 1))

            @pl.when(t == 1)
            def _():
                ring.start(bases[3], w2_src(layer, 0))

            normalize(h, rstd, xn)
            ffn_in(xn, big, ring_buf, base, t, tile, piece, row_piece)

        loop(2, w1_step)

        def w2_step(t):
            base = jnp.where(t == 0, bases[3], bases[4])
            ring.wait(base, w2_src(layer, 0))

            @pl.when(t == 0)
            def _():
                ring.start(bases[4], w2_src(layer, 1))

            if not last:

                @pl.when(t == 1)
                def _():
                    ring.start(bases[5], wo_src(layer + 1))

            ffn_out(h, sums, big, ring_buf, base, t, tile, piece)

        loop(2, w2_step)
        settle_norm(sums, rstd, depth)

    normalize(h, rstd, xn)
    store = block_copies(out_ref, 0, xn, io_sem, to_hbm=True)
    for copy in store:
        copy.start()
    for copy in store:
        copy.wait()


def encoder_call(first_seq, seqs, x, enc_len, wqkv, wo, w1, w2):
    span, depth = x.shape[1], x.shape[2]
    layers, ff = wqkv.shape[0], w1.shape[2]
    rows, tile = seqs * span, depth // 2
    heads = wqkv.shape[3]
    assert ff == 3 * depth and heads * HEAD == depth
    any_spec = pl.BlockSpec(memory_space=pl.ANY)
    per_layer = 2 * rows * depth * (4 * depth + 2 * ff) + 4 * seqs * heads * span * span * HEAD
    return pl.pallas_call(
        functools.partial(encoder_kernel, first_seq * span, seqs, span),
        out_shape=jax.ShapeDtypeStruct((rows, depth), BF16),
        in_specs=[pl.BlockSpec(memory_space=pltpu.SMEM)] + [any_spec] * 5,
        out_specs=any_spec,
        scratch_shapes=[
            pltpu.VMEM((depth // LANES, rows, LANES), BF16),
            pltpu.VMEM((depth // LANES, rows, LANES), BF16),
            pltpu.VMEM((ff // LANES, rows, LANES), BF16),
            pltpu.VMEM((rows, LANES), F32),
            pltpu.VMEM((rows, LANES), F32),
            pltpu.VMEM((3, depth, tile // HEAD, HEAD), BF16),
            pltpu.VMEM((6, depth, tile), BF16),
            pltpu.SemaphoreType.DMA((depth // LANES,)),
            pltpu.SemaphoreType.DMA((3,)),
            pltpu.SemaphoreType.DMA((6,)),
        ],
        compiler_params=pltpu.CompilerParams(vmem_limit_bytes=VMEM_LIMIT),
        cost_estimate=cost(layers * per_layer, 2 * layers * depth * (4 * depth + 2 * ff)),
        name="encode",
    )(enc_len, x.reshape(-1, depth), wqkv, wo.reshape(layers, depth, depth), w1, w2)


def decoder_kernel(first_row, out_row, first_len, seqs, span, len_ref, y_ref, enc_ref, wqkv, wo, wq, wkv, wc, w1, w2, out_ref, z, xn, big, enc, kv, sums, rstd, raw, ring_buf, io_sem, enc_sem, raw_sem, ring_sem):
    layers, depth = wqkv.shape[0], wqkv.shape[1]
    heads = wqkv.shape[3]
    kv_heads = wkv.shape[3]
    rep = heads // kv_heads
    rows = z.shape[1]
    ctx = enc.shape[1] // seqs
    tile = depth // 2
    tile_heads = tile // HEAD
    piece = min(512, tile)
    blocks = depth // LANES
    scale = HEAD**-0.5

    raws = Ring(raw, raw_sem)
    ring = Ring(ring_buf, ring_sem)

    def raw_src(layer, idx):
        if isinstance(idx, int) and idx >= 10:
            return raw_src(layer + 1, idx - 10)
        if isinstance(idx, int) and idx >= 8:
            return [wq.at[layer, :, pl.ds((idx - 8) * tile_heads, tile_heads), :]]
        if isinstance(idx, int) and idx >= 6:
            return [wkv.at[layer, :, idx - 6, :, :]]
        return [wqkv.at[layer, :, idx // 2, pl.ds(pl.multiple_of(lax.rem(idx, 2) * tile_heads, tile_heads), tile_heads), :]]

    def wo_src(layer):
        return [wo.at[layer, :, pl.ds(n * tile, tile)] for n in range(2)]

    def wc_src(layer):
        return [wc.at[layer, :, pl.ds(n * tile, tile)] for n in range(2)]

    def w1_src(layer, t):
        return [w1.at[layer, :, pl.ds((t * 3 + k) * tile, tile)] for k in range(3)]

    def w2_src(layer, t):
        return [w2.at[layer, pl.ds(k * depth, depth), pl.ds(t * tile, tile)] for k in range(3)]

    def project(dst, first, lhs, slot, wide):
        w = raw[slot].reshape(depth, tile)
        for n in range(tile // wide):
            put_blocks(dst, first + n * wide // LANES, dot(joined(lhs, range(blocks)), w[:, n * wide : (n + 1) * wide]).astype(BF16))

    def add_out(base):
        for k in range(2):
            for n in range(tile // piece):
                add_to_state(z, sums, (k * tile + n * piece) // LANES, dot(joined(xn, range(blocks)), ring_buf[base + k, :, n * piece : (n + 1) * piece]))

    load = block_copies(y_ref, first_row, z, io_sem)
    load_enc = block_copies(enc_ref, 0, enc, enc_sem)
    for copy in load:
        copy.start()
    raws.start(0, raw_src(0, 0))
    load_state(load, z, sums)
    settle_norm(sums, rstd, depth)
    raws.start(1, raw_src(0, 1))
    raws.start(2, raw_src(0, 2))
    ring.start(0, wo_src(0))

    for layer in range(layers):
        last = layer + 1 == layers
        shift = 10 * layer % 4
        bases = [((6 * layer + g) % 2) * 3 for g in range(7)]

        def raw_slot(idx):
            return (shift + idx) % 4

        def raw_ahead(idx):
            if idx + 3 < 10 or not last:
                raws.start(raw_slot(idx + 3), raw_src(layer, idx + 3))

        def qkv_step(j):
            slot = lax.rem(j + shift, 4)
            raws.wait(slot, raw_src(layer, 0))

            @pl.when(j < 3)
            def _():
                raws.start(lax.rem(j + shift + 3, 4), raw_src(layer, j + 3))

            for later in range(3, 6):

                @pl.when(j == later)
                def _(later=later):
                    raw_ahead(later)

            project(big, j * (tile // LANES), xn, slot, tile)

        normalize(z, rstd, xn)
        loop(6, qkv_step)

        if layer == 0:
            for copy in load_enc:
                copy.start()

        causal = lax.broadcasted_iota(jnp.int32, (span, span), 1) <= lax.broadcasted_iota(jnp.int32, (span, span), 0)

        def self_step(b):
            at = pl.ds(pl.multiple_of(b * span, span), span)

            def scores(u):
                return jnp.where(causal, dot_t(big[u, at], big[heads + u, at]), -1e30 / scale)

            def finish(u, probs):
                xn[u, at] = dot(probs, big[2 * heads + u, at]).astype(BF16)

            attend_units(heads, scores, scale, finish)

        loop(seqs, self_step)

        ring.wait(bases[0], wo_src(layer))
        ring.start(bases[1], wc_src(layer))
        add_out(bases[0])
        settle_norm(sums, rstd, depth)

        if layer == 0:
            for copy in load_enc:
                copy.wait()
        def kv_step(t):
            slot = lax.rem(t + shift + 6, 4)
            raws.wait(slot, raw_src(layer, 6))
            for later in range(2):

                @pl.when(t == later)
                def _(later=later):
                    raw_ahead(6 + later)

            project(kv, t * (tile // LANES), enc, slot, piece)

        loop(2, kv_step)

        def cross_q_step(t):
            slot = lax.rem(t + shift + 8, 4)
            raws.wait(slot, raw_src(layer, 8))
            for later in range(2):

                @pl.when(t == later)
                def _(later=later):
                    raw_ahead(8 + later)

            project(big, t * (tile // LANES), xn, slot, tile)

        normalize(z, rstd, xn)
        loop(2, cross_q_step)

        def cross_step(b):
            at = pl.ds(pl.multiple_of(b * span, span), span)
            at_kv = pl.ds(pl.multiple_of(b * ctx, ctx), ctx)
            keep = lax.broadcasted_iota(jnp.int32, (1, ctx), 1) < len_ref[b + first_len]

            def scores(g):
                query = jnp.concatenate([big[g * rep + r, at] for r in range(rep)], axis=0)
                return jnp.where(keep, dot_t(query, kv[g, at_kv]), -1e30 / scale)

            def finish(g, probs):
                mixed = dot(probs, kv[kv_heads + g, at_kv]).astype(BF16)
                for r in range(rep):
                    xn[g * rep + r, at] = mixed[r * span : (r + 1) * span]

            attend_units(kv_heads, scores, scale, finish)

        loop(seqs, cross_step)

        ring.wait(bases[1], wc_src(layer))
        ring.start(bases[2], w1_src(layer, 0))
        add_out(bases[1])
        settle_norm(sums, rstd, depth)

        def w1_step(t):
            base = jnp.where(t == 0, bases[2], bases[3])
            ring.wait(base, w1_src(layer, 0))

            @pl.when(t == 0)
            def _():
                ring.start(bases[3], w1_src(layer, 1))

            @pl.when(t == 1)
            def _():
                ring.start(bases[4], w2_src(layer, 0))

            ffn_in(xn, big, ring_buf, base, t, tile, piece, rows)

        normalize(z, rstd, xn)
        loop(2, w1_step)

        def w2_step(t):
            base = jnp.where(t == 0, bases[4], bases[5])
            ring.wait(base, w2_src(layer, 0))

            @pl.when(t == 0)
            def _():
                ring.start(bases[5], w2_src(layer, 1))

            if not last:

                @pl.when(t == 1)
                def _():
                    ring.start(bases[6], wo_src(layer + 1))

            ffn_out(z, sums, big, ring_buf, base, t, tile, piece)

        loop(2, w2_step)
        if not last:
            settle_norm(sums, rstd, depth)

    store = block_copies(out_ref, out_row, z, io_sem, to_hbm=True)
    for copy in store:
        copy.start()
    for copy in store:
        copy.wait()


def decoder_call(first_seq, seqs, y, first_len, enc_len, enc, out_seq, out_seqs, wqkv, wo, wq, wkv, wc, w1, w2):
    span, depth = y.shape[1], y.shape[2]
    layers, ff = wqkv.shape[0], w1.shape[2]
    heads = wqkv.shape[3]
    rows, tile, ctx = seqs * span, depth // 2, enc.shape[0]
    assert ff == 3 * depth and heads * HEAD == depth
    any_spec = pl.BlockSpec(memory_space=pl.ANY)
    per_layer = 2 * rows * depth * (6 * depth + 2 * ff) + 4 * ctx * depth * depth + 4 * seqs * heads * span * (span + ctx // seqs) * HEAD
    return pl.pallas_call(
        functools.partial(decoder_kernel, first_seq * span, out_seq * span, first_len, seqs, span),
        out_shape=jax.ShapeDtypeStruct((out_seqs * span, depth), BF16),
        in_specs=[pl.BlockSpec(memory_space=pltpu.SMEM)] + [any_spec] * 9,
        out_specs=any_spec,
        scratch_shapes=[
            pltpu.VMEM((depth // LANES, rows, LANES), BF16),
            pltpu.VMEM((depth // LANES, rows, LANES), BF16),
            pltpu.VMEM((ff // LANES, rows, LANES), BF16),
            pltpu.VMEM((depth // LANES, ctx, LANES), BF16),
            pltpu.VMEM((depth // LANES, ctx, LANES), BF16),
            pltpu.VMEM((rows, LANES), F32),
            pltpu.VMEM((rows, LANES), F32),
            pltpu.VMEM((4, depth, tile // HEAD, HEAD), BF16),
            pltpu.VMEM((6, depth, tile), BF16),
            pltpu.SemaphoreType.DMA((depth // LANES,)),
            pltpu.SemaphoreType.DMA((depth // LANES,)),
            pltpu.SemaphoreType.DMA((4,)),
            pltpu.SemaphoreType.DMA((6,)),
        ],
        compiler_params=pltpu.CompilerParams(vmem_limit_bytes=VMEM_LIMIT),
        cost_estimate=cost(layers * per_layer, 2 * layers * depth * (8 * depth + 2 * ff)),
        name="decode",
    )(
        enc_len,
        y.reshape(-1, depth),
        enc,
        wqkv,
        wo.reshape(layers, depth, depth),
        wq.reshape(layers, depth, heads, HEAD),
        wkv,
        wc.reshape(layers, depth, depth),
        w1,
        w2,
    )


def solution(mesh):
    stages = mesh.shape["stage"]
    swap = [(source, (source + stages // 2) % stages) for source in range(stages)]
    rows = P(("data", "stage"))
    whole = P()

    def body(x_enc, enc_len, y, enc_wqkv, enc_wo, enc_w1, enc_w2, dec_wqkv, dec_wo, cross_wq, cross_wkv, cross_wo, dec_w1, dec_w2):
        seqs, span, depth = y.shape
        half = seqs // 2
        enc_weights = (enc_wqkv, enc_wo, enc_w1, enc_w2)
        dec_weights = (dec_wqkv, dec_wo, cross_wq, cross_wkv, cross_wo, dec_w1, dec_w2)

        y_recv = lax.ppermute(y, "stage", swap)
        len_recv = lax.ppermute(enc_len, "stage", swap)
        home_enc = encoder_call(half, half, x_enc, enc_len, *enc_weights)
        home_recv = lax.ppermute(home_enc, "stage", swap)
        x_next, _ = lax.optimization_barrier((x_enc, home_enc))
        away_enc = encoder_call(0, half, x_next, enc_len, *enc_weights)
        away_out = decoder_call(0, half, y_recv, 0, enc_len, away_enc, 0, half, *dec_weights)
        out_recv = lax.ppermute(away_out, "stage", swap)
        y_next, _ = lax.optimization_barrier((y, away_out))
        home_out = decoder_call(half, half, y_next, half, len_recv, home_recv, half, seqs, *dec_weights)
        return lax.dynamic_update_slice(home_out, out_recv, (0, 0)).reshape(y.shape)

    return jax.shard_map(body, mesh=mesh, in_specs=(rows, rows, rows) + (whole,) * 11, out_specs=rows, check_vma=False)
```

time: 1740 us -> 734 us (0.42)
  matrix products: 891 us -> 0 us
  Pallas kernels: 0 us -> 708 us
  waiting for transfers between devices: 614 us -> 0.01 us
  other arithmetic: 113 us -> 0 us
  local copies, waits for them, and re-layouts: 100 us -> 2.73 us
    dot_general x27 -> x0, matrix products: 891 us -> none  [the longest x4 197 us: ffn_block(): jnp.einsum('bsd,df->bsf', rms_norm(state), w_in, preferred_element_type=j...]
    pallas_call x0 -> x4, Pallas kernels: none -> 708 us  [the longest x2 444 us: encoder_call(): pl.pallas_call(functools.partial(encoder_kernel, first_seq * span, seqs,...]
    ppermute x1, waiting for transfers between devices: 614 us -> 0.01 us  [body(): len_recv = lax.ppermute(enc_len, 'stage', swap)]
    slice x2 -> x0, local copies, waits for them, and re-layouts: 70.8 us -> none  [the longest x1 35.7 us: decoder(): state = self_block(state, dec_wqkv[layer], dec_wo[layer], causal)]
    reduce_sum x6 -> x0, other arithmetic: 56.3 us -> none  [the longest x4 50.5 us: attend(): jax.nn.softmax(jnp.where(valid, scores, -1e+30), axis=-1)]
    sub x2 -> x0, other arithmetic: 55.8 us -> none  [attend(): jax.nn.softmax(jnp.where(valid, scores, -1e+30), axis=-1)]
  transfers between devices with their start and end apart: 2 -> 4, of which waited for: 1 -> 0; matrix products, arithmetic and copies ran while one was open for 6% -> 0% of each run, Pallas kernels for 0% -> 98%
where the time goes in v1:
time: 734 us; the launch traced here: 726 us
  Pallas kernels  708 us (96%)
  starting transfers between devices  14.2 us (2%)
    pallas_call x2, Pallas kernels, encoder_call(): pl.pallas_call(functools.partial(encoder_kernel, first_seq * span, seqs,...  444 us
    pallas_call x2, Pallas kernels, decoder_call(): pl.pallas_call(functools.partial(decoder_kernel, first_seq * span, out_se...  265 us
  transfers between devices with their start and end apart: 4, of which 0 were waited for; matrix products, arithmetic and copies ran while one was open for 0% of the time, Pallas kernels for 98%

profile of v1, /device:TPU:28, one launch (start us, length us, event | category | flops | bytes accessed | tf_op | source)
XLA Modules:
  0.0 725.7 jit_solution(16957913726277628509)
XLA Ops:
  0.0 8.0 %collective-permute-start.1 = (bf16[4,192,2048]{2,1,0:T(8,128)(2,1)}, bf16[4,192,2048]{2,1,0:T(8,128)(2,1)}, u32[]{:S(2)}, u32[]{:S(2)}) collective-permute-start(bf16[4,192,2048]{2,1,0:T(8,128)(2,1)} %param.16), channel_id=1, source_target_pairs={{0,8},{1,9},{2,10},{3,11},{4,12},{5,13},{6,14},{7,15},{8,0},{9,1},... | collective-permute-start | bytes 9437192 | tf_op jit(solution)/shard_map/ppermute | solution.py:591
  8.0 0.0 collective-permute-start
  8.0 221.9 %encode.2 = bf16[1024,2048]{1,0:T(8,128)(2,1)} custom-call(s32[4]{0:T(128)} %len_ref.5, bf16[2048,2048]{1,0:T(8,128)(2,1)} %bitcast.17, bf16[2,2048,3,16,128]{4,3,2,1,0:T(8,128)(2,1)} %wqkv.5, bf16[2,2048,2048]{2,1,0:T(8,128)(2,1)} %bitcast.9, bf16[2,2048,6144]{2,1,0:T(8,128)(2,1)} %w1.5, bf16[2,6144,2048]{2,1,0:T(8,128)(2,1)} %w2.5), custom_call_target="tpu_custom_call" | custom-call | flops 180388626432 | bytes 167772160 | tf_op jit(solution)/shard_map/encode/pallas_call | solution.py:301
  230.0 6.0 collective-permute-start.2
  236.0 222.0 %encode.3.enc_ref = bf16[1024,2048]{1,0:T(8,128)(2,1)} custom-call(s32[4]{0:T(128)} %len_ref.5, bf16[2048,2048]{1,0:T(8,128)(2,1)} %bitcast.18, bf16[2,2048,3,16,128]{4,3,2,1,0:T(8,128)(2,1)} %wqkv.5, bf16[2,2048,2048]{2,1,0:T(8,128)(2,1)} %bitcast.10, bf16[2,2048,6144]{2,1,0:T(8,128)(2,1)} %w1.5, bf16[2,6144,2048]{2,1,0:T(8,128)(2,1)} %w2.5), custom_call_target="tpu_custom_call" | custom-call | flops 180388626432 | bytes 167772160 | tf_op jit(solution)/shard_map/encode/pallas_call | solution.py:301
  458.0 0.0 collective-permute-done.1
  458.0 132.5 %decode.2 = bf16[384,2048]{1,0:T(8,128)(2,1)} custom-call(s32[4]{0:T(128)} %len_ref.5, bf16[768,2048]{1,0:T(8,128)(2,1)} %bitcast.y_ref, bf16[1024,2048]{1,0:T(8,128)(2,1)} %encode.3.enc_ref, bf16[2,2048,3,16,128]{4,3,2,1,0:T(8,128)(2,1)} %wqkv.7, bf16[2,2048,2048]{2,1,0:T(8,128)(2,1)} %bitcast.11, bf16[2,2048,16,128]{3,2,1,0:T(8,128)(2,1)} %bitcast.13, ...), custom_call_target="tpu_custom_call" | custom-call | flops 116098334720 | bytes 234881024 | tf_op jit(solution)/shard_map/decode/pallas_call | solution.py:542
  590.5 0.1 collective-permute-start.3
  590.6 0.0 collective-permute-done.len_ref
  590.6 0.0 collective-permute-done.2.enc_ref
  590.7 132.0 %decode.3 = bf16[768,2048]{1,0:T(8,128)(2,1)} custom-call(s32[4]{0:T(128)} %collective-permute-done.len_ref, bf16[768,2048]{1,0:T(8,128)(2,1)} %bitcast.19, bf16[1024,2048]{1,0:T(8,128)(2,1)} %collective-permute-done.2.enc_ref, bf16[2,2048,3,16,128]{4,3,2,1,0:T(8,128)(2,1)} %wqkv.7, bf16[2,2048,2048]{2,1,0:T(8,128)(2,1)} %bitcast.12, ...), custom_call_target="tpu_custom_call" | custom-call | flops 116098334720 | bytes 234881024 | tf_op jit(solution)/shard_map/decode/pallas_call | solution.py:542
  722.7 0.0 collective-permute-done.3
  722.7 2.7 constant_dynamic-update-slice_fusion
Async XLA Ops:
  0.0 458.0 %collective-permute-start.1 = (bf16[4,192,2048]{2,1,0:T(8,128)(2,1)}, bf16[4,192,2048]{2,1,0:T(8,128)(2,1)}, u32[]{:S(2)}, u32[]{:S(2)}) collective-permute-start(bf16[4,192,2048]{2,1,0:T(8,128)(2,1)} %param.16), channel_id=1, source_target_pairs={{0,8},{1,9},{2,10},{3,11},{4,12},{5,13},{6,14},{7,15},{8,0},{9,1},... | collective-permute-start | bytes 9437192 | tf_op jit(solution)/shard_map/ppermute | solution.py:591
  8.0 582.6 %collective-permute-start = (s32[4]{0:T(128)}, s32[4]{0:T(128)}, u32[]{:S(2)}, u32[]{:S(2)}) collective-permute-start(s32[4]{0:T(128)} %len_ref.5), channel_id=1, source_target_pairs={{0,8},{1,9},{2,10},{3,11},{4,12},{5,13},{6,14},{7,15},{8,0},{9,1},... | collective-permute-start | bytes 56 | tf_op jit(solution)/shard_map/ppermute | solution.py:592
  230.0 360.7 %collective-permute-start.2 = (bf16[1024,2048]{1,0:T(8,128)(2,1)}, bf16[1024,2048]{1,0:T(8,128)(2,1)}, u32[]{:S(2)}, u32[]{:S(2)}) collective-permute-start(bf16[1024,2048]{1,0:T(8,128)(2,1)} %encode.2), channel_id=1, source_target_pairs={{0,8},{1,9},{2,10},{3,11},{4,12},{5,13},{6,14},{7,15},{8,0},{9,1},... | collective-permute-start | bytes 12582920 | tf_op jit(solution)/shard_map/ppermute | solution.py:594
  590.5 132.2 %collective-permute-start.3 = (bf16[384,2048]{1,0:T(8,128)(2,1)}, bf16[384,2048]{1,0:T(8,128)(2,1)}, u32[]{:S(2)}, u32[]{:S(2)}) collective-permute-start(bf16[384,2048]{1,0:T(8,128)(2,1)} %decode.2), channel_id=1, source_target_pairs={{0,8},{1,9},{2,10},{3,11},{4,12},{5,13},{6,14},{7,15},{8,0},{9,1},... | collective-permute-start | bytes 4718600 | tf_op jit(solution)/shard_map/ppermute | solution.py:598

commit v2 on v1

--- a/solution.py
+++ b/solution.py
@@ -36,12 +36,17 @@
     return (weight * (1.0 / total)).astype(BF16)
 
 
-def attend_units(count, make_scores, scale, finish):
+def attend_units(count, make_scores, scale, finish, filler=()):
+    done = 0
     ahead = make_scores(0)
     for i in range(count):
         now = ahead
         if i + 1 < count:
             ahead = make_scores(i + 1)
+        upto = len(filler) * (i + 1) // count
+        for piece in filler[done:upto]:
+            piece()
+        done = upto
         finish(i, softmax_rows(now, scale))
 
 
@@ -68,14 +73,14 @@
         dst[c] = (state[c].astype(F32) * rstd[...]).astype(BF16)
 
 
-def add_to_state(state, sums, first, update):
+def add_to_state(state, sums, first, update, rows=slice(None)):
     part = None
     for k in range(update.shape[1] // LANES):
-        fresh = (state[first + k].astype(F32) + update[:, k * LANES : (k + 1) * LANES]).astype(BF16)
-        state[first + k] = fresh
+        fresh = (state[first + k, rows].astype(F32) + update[:, k * LANES : (k + 1) * LANES]).astype(BF16)
+        state[first + k, rows] = fresh
         wide = fresh.astype(F32)
         part = wide * wide if part is None else part + wide * wide
-    sums[...] += part
+    sums[rows] += part
 
 
 def put_blocks(dst, first, value, rows=slice(None)):
@@ -94,19 +99,25 @@
 
 
 class Ring:
-    def __init__(self, buf, sem):
-        self.buf, self.sem = buf, sem
-
-    def copies(self, base, refs):
-        return [pltpu.make_async_copy(ref, self.buf.at[base + k], self.sem.at[base + k]) for k, ref in enumerate(refs)]
+    def __init__(self, buf, sem, split=False):
+        self.buf, self.sem, self.split = buf, sem, split
 
     def start(self, base, refs):
-        for copy in self.copies(base, refs):
-            copy.start()
+        for k, ref in enumerate(refs):
+            if self.split:
+                for c in range(self.buf.shape[1]):
+                    pltpu.make_async_copy(ref.at[:, pl.ds(c * LANES, LANES)], self.buf.at[base + k, c], self.sem.at[base + k]).start()
+            else:
+                pltpu.make_async_copy(ref, self.buf.at[base + k], self.sem.at[base + k]).start()
 
     def wait(self, base, refs):
-        for copy in self.copies(base, refs):
-            copy.wait()
+        for k in range(len(refs)):
+            slot = self.buf.at[base + k]
+            pltpu.make_async_copy(slot, slot, self.sem.at[base + k]).wait()
+
+
+def ring_cols(ring, slot, first, width):
+    return jnp.concatenate([ring[slot, first // LANES + c] for c in range(width // LANES)], axis=1)
 
 
 def at_cols(i, width):
@@ -133,10 +144,9 @@
 
 def ffn_in(xn, big, ring, base, t, tile, piece, row_piece):
     blocks = range(xn.shape[0])
-    per = piece // LANES
     for k in range(3):
         for n in range(tile // piece):
-            w = ring[base + k, :, n * piece : (n + 1) * piece]
+            w = ring_cols(ring, base + k, n * piece, piece)
             for m in range(xn.shape[1] // row_piece):
                 rows = slice(m * row_piece, (m + 1) * row_piece)
                 put_blocks(big, t * (3 * tile // LANES) + (k * tile + n * piece) // LANES, gelu(dot(joined(xn, blocks, rows), w)).astype(BF16), rows)
@@ -147,7 +157,7 @@
     for n in range(tile // piece):
         total = None
         for k in range(3):
-            part = dot(joined(big, range(k * depth_blocks, (k + 1) * depth_blocks)), ring[base + k, :, n * piece : (n + 1) * piece])
+            part = dot(joined(big, range(k * depth_blocks, (k + 1) * depth_blocks)), ring_cols(ring, base + k, n * piece, piece))
             total = part if total is None else total + part
         add_to_state(state, sums, t * (tile // LANES) + n * piece // LANES, total)
 
@@ -163,13 +173,13 @@
     tile = depth // 2
     tile_heads = tile // HEAD
     piece = min(512, tile)
-    row_piece = min(512, rows)
+    row_piece = min(256, rows)
     blocks = depth // LANES
     n_qkv = 6
     scale = HEAD**-0.5
 
     raws = Ring(raw, raw_sem)
-    ring = Ring(ring_buf, ring_sem)
+    ring = Ring(ring_buf, ring_sem, split=True)
 
     def qkv_src(layer, j):
         return [wqkv.at[layer, :, j // 2, pl.ds(pl.multiple_of(lax.rem(j, 2) * tile_heads, tile_heads), tile_heads), :]]
@@ -189,7 +199,6 @@
     raws.start(0, qkv_src(0, 0))
     load_state(load, h, sums)
     settle_norm(sums, rstd, depth)
-    raws.start(1, qkv_src(0, 1))
     ring.start(0, wo_src(0))
 
     for layer in range(layers):
@@ -197,18 +206,18 @@
         bases = [((5 * layer + g) % 2) * 3 for g in range(6)]
 
         def qkv_step(j):
-            slot = lax.rem(j, 3)
+            slot = lax.rem(j, 2)
             raws.wait(slot, qkv_src(layer, j))
 
-            @pl.when(j < n_qkv - 2)
-            def _():
-                raws.start(lax.rem(j + 2, 3), qkv_src(layer, j + 2))
+            @pl.when(j < n_qkv - 1)
+            def _():
+                raws.start(1 - slot, qkv_src(layer, j + 1))
 
             if not last:
 
-                @pl.when(j >= n_qkv - 2)
+                @pl.when(j == n_qkv - 1)
                 def _():
-                    raws.start(lax.rem(j + 2, 3), qkv_src(layer + 1, j + 2 - n_qkv))
+                    raws.start(0, qkv_src(layer + 1, 0))
 
             normalize(h, rstd, xn)
             w = raw[slot].reshape(depth, tile)
@@ -217,33 +226,36 @@
 
         loop(n_qkv, qkv_step)
 
+        def attention(b, at, first_head, count, filler=()):
+            keep = lax.broadcasted_iota(jnp.int32, (1, span), 1) < len_ref[b + first_row // span]
+
+            def scores(u):
+                return jnp.where(keep, dot_t(big[first_head + u, at], big[heads + first_head + u, at]), -1e30 / scale)
+
+            def finish(u, probs):
+                xn[first_head + u, at] = dot(probs, big[2 * heads + first_head + u, at]).astype(BF16)
+
+            attend_units(count, scores, scale, finish, filler)
+
         def attend_step(i):
             groups = heads // tile_heads
             b, g = i // groups, lax.rem(i, groups)
-            keep = lax.broadcasted_iota(jnp.int32, (1, span), 1) < len_ref[b + first_row // span]
-            at = pl.ds(pl.multiple_of(b * span, span), span)
-
-            def head(u, which):
-                return which * heads + g * tile_heads + u
-
-            def scores(u):
-                return jnp.where(keep, dot_t(big[head(u, 0), at], big[head(u, 1), at]), -1e30 / scale)
-
-            def finish(u, probs):
-                xn[head(u, 0), at] = dot(probs, big[head(u, 2), at]).astype(BF16)
-
-            attend_units(tile_heads, scores, scale, finish)
-
-        loop(seqs * (heads // tile_heads), attend_step)
+            attention(b, pl.ds(pl.multiple_of(b * span, span), span), g * tile_heads, tile_heads)
+
+        loop((seqs - 1) * (heads // tile_heads), attend_step)
+
+        def out_piece(n, at):
+            w = ring_cols(ring_buf, bases[0] + n * piece // tile, (n * piece) % tile, piece)
+            add_to_state(h, sums, n * piece // LANES, dot(joined(xn, range(blocks), at), w), at)
 
         ring.wait(bases[0], wo_src(layer))
         ring.start(bases[1], w1_src(layer, 0))
-
-        def wo_step(t):
-            for n in range(tile // piece):
-                add_to_state(h, sums, t * (tile // LANES) + n * piece // LANES, dot(joined(xn, range(blocks)), ring_buf[bases[0] + t, :, n * piece : (n + 1) * piece]))
-
-        loop(2, wo_step)
+        n_out = depth // piece
+        before = [slice(b * span, (b + 1) * span) for b in range(seqs - 1)]
+        final = slice((seqs - 1) * span, seqs * span)
+        attention(seqs - 1, final, 0, heads, [functools.partial(out_piece, n, at) for at in before for n in range(n_out)])
+        for n in range(n_out):
+            out_piece(n, final)
         settle_norm(sums, rstd, depth)
 
         def w1_step(t):
@@ -309,10 +321,10 @@
             pltpu.VMEM((ff // LANES, rows, LANES), BF16),
             pltpu.VMEM((rows, LANES), F32),
             pltpu.VMEM((rows, LANES), F32),
-            pltpu.VMEM((3, depth, tile // HEAD, HEAD), BF16),
-            pltpu.VMEM((6, depth, tile), BF16),
+            pltpu.VMEM((2, depth, tile // HEAD, HEAD), BF16),
+            pltpu.VMEM((6, tile // LANES, depth, LANES), BF16),
             pltpu.SemaphoreType.DMA((depth // LANES,)),
-            pltpu.SemaphoreType.DMA((3,)),
+            pltpu.SemaphoreType.DMA((2,)),
             pltpu.SemaphoreType.DMA((6,)),
         ],
         compiler_params=pltpu.CompilerParams(vmem_limit_bytes=VMEM_LIMIT),
@@ -335,7 +347,7 @@
     scale = HEAD**-0.5
 
     raws = Ring(raw, raw_sem)
-    ring = Ring(ring_buf, ring_sem)
+    ring = Ring(ring_buf, ring_sem, split=True)
 
     def raw_src(layer, idx):
         if isinstance(idx, int) and idx >= 10:
@@ -363,10 +375,14 @@
         for n in range(tile // wide):
             put_blocks(dst, first + n * wide // LANES, dot(joined(lhs, range(blocks)), w[:, n * wide : (n + 1) * wide]).astype(BF16))
 
-    def add_out(base):
-        for k in range(2):
-            for n in range(tile // piece):
-                add_to_state(z, sums, (k * tile + n * piece) // LANES, dot(joined(xn, range(blocks)), ring_buf[base + k, :, n * piece : (n + 1) * piece]))
+    def out_piece(base, n, at):
+        w = ring_cols(ring_buf, base + n * piece // tile, (n * piece) % tile, piece)
+        add_to_state(z, sums, n * piece // LANES, dot(joined(xn, range(blocks), at), w), at)
+
+    n_out = depth // piece
+    every = slice(0, rows)
+    before = [slice(b * span, (b + 1) * span) for b in range(seqs - 1)]
+    final = slice((seqs - 1) * span, seqs * span)
 
     load = block_copies(y_ref, first_row, z, io_sem)
     load_enc = block_copies(enc_ref, 0, enc, enc_sem)
@@ -376,30 +392,29 @@
     load_state(load, z, sums)
     settle_norm(sums, rstd, depth)
     raws.start(1, raw_src(0, 1))
-    raws.start(2, raw_src(0, 2))
     ring.start(0, wo_src(0))
 
     for layer in range(layers):
         last = layer + 1 == layers
-        shift = 10 * layer % 4
+        shift = 10 * layer % 3
         bases = [((6 * layer + g) % 2) * 3 for g in range(7)]
 
         def raw_slot(idx):
-            return (shift + idx) % 4
+            return (shift + idx) % 3
 
         def raw_ahead(idx):
-            if idx + 3 < 10 or not last:
-                raws.start(raw_slot(idx + 3), raw_src(layer, idx + 3))
+            if idx + 2 < 10 or not last:
+                raws.start(raw_slot(idx + 2), raw_src(layer, idx + 2))
 
         def qkv_step(j):
-            slot = lax.rem(j + shift, 4)
+            slot = lax.rem(j + shift, 3)
             raws.wait(slot, raw_src(layer, 0))
 
-            @pl.when(j < 3)
-            def _():
-                raws.start(lax.rem(j + shift + 3, 4), raw_src(layer, j + 3))
-
-            for later in range(3, 6):
+            @pl.when(j < 4)
+            def _():
+                raws.start(lax.rem(j + shift + 2, 3), raw_src(layer, j + 2))
+
+            for later in range(4, 6):
 
                 @pl.when(j == later)
                 def _(later=later):
@@ -408,50 +423,53 @@
             project(big, j * (tile // LANES), xn, slot, tile)
 
         normalize(z, rstd, xn)
-        loop(6, qkv_step)
-
         if layer == 0:
             for copy in load_enc:
                 copy.start()
-
-        causal = lax.broadcasted_iota(jnp.int32, (span, span), 1) <= lax.broadcasted_iota(jnp.int32, (span, span), 0)
-
-        def self_step(b):
-            at = pl.ds(pl.multiple_of(b * span, span), span)
-
-            def scores(u):
-                return jnp.where(causal, dot_t(big[u, at], big[heads + u, at]), -1e30 / scale)
-
-            def finish(u, probs):
-                xn[u, at] = dot(probs, big[2 * heads + u, at]).astype(BF16)
-
-            attend_units(heads, scores, scale, finish)
-
-        loop(seqs, self_step)
-
-        ring.wait(bases[0], wo_src(layer))
-        ring.start(bases[1], wc_src(layer))
-        add_out(bases[0])
-        settle_norm(sums, rstd, depth)
+        loop(6, qkv_step)
 
         if layer == 0:
             for copy in load_enc:
                 copy.wait()
-        def kv_step(t):
-            slot = lax.rem(t + shift + 6, 4)
+
+        causal = lax.broadcasted_iota(jnp.int32, (span, span), 1) <= lax.broadcasted_iota(jnp.int32, (span, span), 0)
+
+        def self_step(b):
+            slot = lax.rem(b + shift + 6, 3)
             raws.wait(slot, raw_src(layer, 6))
             for later in range(2):
 
-                @pl.when(t == later)
+                @pl.when(b == later)
                 def _(later=later):
                     raw_ahead(6 + later)
 
-            project(kv, t * (tile // LANES), enc, slot, piece)
-
-        loop(2, kv_step)
+            at = pl.ds(pl.multiple_of(b * span, span), span)
+            w = raw[slot].reshape(depth, tile)
+            kv_rows = min(256, kv.shape[1])
+
+            def kv_piece(n, m):
+                part = slice(m * kv_rows, (m + 1) * kv_rows)
+                put_blocks(kv, b * (tile // LANES) + n * piece // LANES, dot(joined(enc, range(blocks), part), w[:, n * piece : (n + 1) * piece]).astype(BF16), part)
+
+            def scores(u):
+                return jnp.where(causal, dot_t(big[u, at], big[heads + u, at]), -1e30 / scale)
+
+            def finish(u, probs):
+                xn[u, at] = dot(probs, big[2 * heads + u, at]).astype(BF16)
+
+            pieces = [functools.partial(kv_piece, n, m) for n in range(tile // piece) for m in range(kv.shape[1] // kv_rows)]
+            attend_units(heads, scores, scale, finish, pieces)
+
+        loop(2, self_step)
+
+        ring.wait(bases[0], wo_src(layer))
+        ring.start(bases[1], wc_src(layer))
+        for n in range(n_out):
+            out_piece(bases[0], n, every)
+        settle_norm(sums, rstd, depth)
 
         def cross_q_step(t):
-            slot = lax.rem(t + shift + 8, 4)
+            slot = lax.rem(t + shift + 8, 3)
             raws.wait(slot, raw_src(layer, 8))
             for later in range(2):
 
@@ -464,9 +482,7 @@
         normalize(z, rstd, xn)
         loop(2, cross_q_step)
 
-        def cross_step(b):
-            at = pl.ds(pl.multiple_of(b * span, span), span)
-            at_kv = pl.ds(pl.multiple_of(b * ctx, ctx), ctx)
+        def cross(b, at, at_kv, filler=()):
             keep = lax.broadcasted_iota(jnp.int32, (1, ctx), 1) < len_ref[b + first_len]
 
             def scores(g):
@@ -478,13 +494,16 @@
                 for r in range(rep):
                     xn[g * rep + r, at] = mixed[r * span : (r + 1) * span]
 
-            attend_units(kv_heads, scores, scale, finish)
-
-        loop(seqs, cross_step)
+            attend_units(kv_heads, scores, scale, finish, filler)
 
         ring.wait(bases[1], wc_src(layer))
         ring.start(bases[2], w1_src(layer, 0))
-        add_out(bases[1])
+        for b in range(seqs - 1):
+            cross(b, before[b], slice(b * ctx, (b + 1) * ctx))
+        pieces = [functools.partial(out_piece, bases[1], n, at) for at in before for n in range(n_out)]
+        cross(seqs - 1, final, slice((seqs - 1) * ctx, seqs * ctx), pieces)
+        for n in range(n_out):
+            out_piece(bases[1], n, final)
         settle_norm(sums, rstd, depth)
 
         def w1_step(t):
@@ -499,7 +518,7 @@
             def _():
                 ring.start(bases[4], w2_src(layer, 0))
 
-            ffn_in(xn, big, ring_buf, base, t, tile, piece, rows)
+            ffn_in(xn, big, ring_buf, base, t, tile, tile, rows // 2)
 
         normalize(z, rstd, xn)
         loop(2, w1_step)
@@ -536,7 +555,7 @@
     layers, ff = wqkv.shape[0], w1.shape[2]
     heads = wqkv.shape[3]
     rows, tile, ctx = seqs * span, depth // 2, enc.shape[0]
-    assert ff == 3 * depth and heads * HEAD == depth
+    assert ff == 3 * depth and heads * HEAD == depth and seqs == 2
     any_spec = pl.BlockSpec(memory_space=pl.ANY)
     per_layer = 2 * rows * depth * (6 * depth + 2 * ff) + 4 * ctx * depth * depth + 4 * seqs * heads * span * (span + ctx // seqs) * HEAD
     return pl.pallas_call(
@@ -552,11 +571,11 @@
             pltpu.VMEM((depth // LANES, ctx, LANES), BF16),
             pltpu.VMEM((rows, LANES), F32),
             pltpu.VMEM((rows, LANES), F32),
-            pltpu.VMEM((4, depth, tile // HEAD, HEAD), BF16),
-            pltpu.VMEM((6, depth, tile), BF16),
+            pltpu.VMEM((3, depth, tile // HEAD, HEAD), BF16),
+            pltpu.VMEM((6, tile // LANES, depth, LANES), BF16),
             pltpu.SemaphoreType.DMA((depth // LANES,)),
             pltpu.SemaphoreType.DMA((depth // LANES,)),
-            pltpu.SemaphoreType.DMA((4,)),
+            pltpu.SemaphoreType.DMA((3,)),
             pltpu.SemaphoreType.DMA((6,)),
         ],
         compiler_params=pltpu.CompilerParams(vmem_limit_bytes=VMEM_LIMIT),

time: 734 us -> 713 us (0.971)
  Pallas kernels: 708 us -> 689 us
    pallas_call x2, Pallas kernels: 444 us -> 430 us  [encoder_call(): pl.pallas_call(functools.partial(encoder_kernel, first_seq * span, seqs,...]
where the time goes in v2:
time: 713 us; the launch traced here: 706 us
  Pallas kernels  689 us (97%)
  starting transfers between devices  14.2 us (2%)
    pallas_call x2, Pallas kernels, encoder_call(): pl.pallas_call(functools.partial(encoder_kernel, first_seq * span, seqs,...  430 us
    pallas_call x2, Pallas kernels, decoder_call(): pl.pallas_call(functools.partial(decoder_kernel, first_seq * span, out_se...  259 us
  transfers between devices with their start and end apart: 4, of which 0 were waited for; matrix products, arithmetic and copies ran while one was open for 0% of the time, Pallas kernels for 98%

profile of v2, /device:TPU:28, one launch (start us, length us, event | category | flops | bytes accessed | tf_op | source)
XLA Modules:
  0.0 706.1 jit_solution(6943613750087293727)
XLA Ops:
  0.0 8.0 %collective-permute-start.1 = (bf16[4,192,2048]{2,1,0:T(8,128)(2,1)}, bf16[4,192,2048]{2,1,0:T(8,128)(2,1)}, u32[]{:S(2)}, u32[]{:S(2)}) collective-permute-start(bf16[4,192,2048]{2,1,0:T(8,128)(2,1)} %param.16), channel_id=1, source_target_pairs={{0,8},{1,9},{2,10},{3,11},{4,12},{5,13},{6,14},{7,15},{8,0},{9,1},... | collective-permute-start | bytes 9437192 | tf_op jit(solution)/shard_map/ppermute | solution.py:610
  8.0 0.0 collective-permute-start
  8.0 214.9 %encode.2 = bf16[1024,2048]{1,0:T(8,128)(2,1)} custom-call(s32[4]{0:T(128)} %len_ref.5, bf16[2048,2048]{1,0:T(8,128)(2,1)} %bitcast.17, bf16[2,2048,3,16,128]{4,3,2,1,0:T(8,128)(2,1)} %wqkv.5, bf16[2,2048,2048]{2,1,0:T(8,128)(2,1)} %bitcast.9, bf16[2,2048,6144]{2,1,0:T(8,128)(2,1)} %w1.5, bf16[2,6144,2048]{2,1,0:T(8,128)(2,1)} %w2.5), custom_call_target="tpu_custom_call" | custom-call | flops 180388626432 | bytes 167772160 | tf_op jit(solution)/shard_map/encode/pallas_call | solution.py:313
  223.0 6.0 collective-permute-start.2
  229.0 214.9 %encode.3.enc_ref = bf16[1024,2048]{1,0:T(8,128)(2,1)} custom-call(s32[4]{0:T(128)} %len_ref.5, bf16[2048,2048]{1,0:T(8,128)(2,1)} %bitcast.18, bf16[2,2048,3,16,128]{4,3,2,1,0:T(8,128)(2,1)} %wqkv.5, bf16[2,2048,2048]{2,1,0:T(8,128)(2,1)} %bitcast.10, bf16[2,2048,6144]{2,1,0:T(8,128)(2,1)} %w1.5, bf16[2,6144,2048]{2,1,0:T(8,128)(2,1)} %w2.5), custom_call_target="tpu_custom_call" | custom-call | flops 180388626432 | bytes 167772160 | tf_op jit(solution)/shard_map/encode/pallas_call | solution.py:313
  443.9 0.0 collective-permute-done.1
  443.9 129.6 %decode.2 = bf16[384,2048]{1,0:T(8,128)(2,1)} custom-call(s32[4]{0:T(128)} %len_ref.5, bf16[768,2048]{1,0:T(8,128)(2,1)} %bitcast.y_ref, bf16[1024,2048]{1,0:T(8,128)(2,1)} %encode.3.enc_ref, bf16[2,2048,3,16,128]{4,3,2,1,0:T(8,128)(2,1)} %wqkv.7, bf16[2,2048,2048]{2,1,0:T(8,128)(2,1)} %bitcast.11, bf16[2,2048,16,128]{3,2,1,0:T(8,128)(2,1)} %bitcast.13, ...), custom_call_target="tpu_custom_call" | custom-call | flops 116098334720 | bytes 234881024 | tf_op jit(solution)/shard_map/decode/pallas_call | solution.py:561
  573.5 0.1 collective-permute-start.3
  573.6 0.0 collective-permute-done.len_ref
  573.6 0.0 collective-permute-done.2.enc_ref
  573.6 129.2 %decode.3 = bf16[768,2048]{1,0:T(8,128)(2,1)} custom-call(s32[4]{0:T(128)} %collective-permute-done.len_ref, bf16[768,2048]{1,0:T(8,128)(2,1)} %bitcast.19, bf16[1024,2048]{1,0:T(8,128)(2,1)} %collective-permute-done.2.enc_ref, bf16[2,2048,3,16,128]{4,3,2,1,0:T(8,128)(2,1)} %wqkv.7, bf16[2,2048,2048]{2,1,0:T(8,128)(2,1)} %bitcast.12, ...), custom_call_target="tpu_custom_call" | custom-call | flops 116098334720 | bytes 234881024 | tf_op jit(solution)/shard_map/decode/pallas_call | solution.py:561
  702.8 0.0 collective-permute-done.3
  702.8 2.7 constant_dynamic-update-slice_fusion
Async XLA Ops:
  0.0 443.9 %collective-permute-start.1 = (bf16[4,192,2048]{2,1,0:T(8,128)(2,1)}, bf16[4,192,2048]{2,1,0:T(8,128)(2,1)}, u32[]{:S(2)}, u32[]{:S(2)}) collective-permute-start(bf16[4,192,2048]{2,1,0:T(8,128)(2,1)} %param.16), channel_id=1, source_target_pairs={{0,8},{1,9},{2,10},{3,11},{4,12},{5,13},{6,14},{7,15},{8,0},{9,1},... | collective-permute-start | bytes 9437192 | tf_op jit(solution)/shard_map/ppermute | solution.py:610
  8.0 565.6 %collective-permute-start = (s32[4]{0:T(128)}, s32[4]{0:T(128)}, u32[]{:S(2)}, u32[]{:S(2)}) collective-permute-start(s32[4]{0:T(128)} %len_ref.5), channel_id=1, source_target_pairs={{0,8},{1,9},{2,10},{3,11},{4,12},{5,13},{6,14},{7,15},{8,0},{9,1},... | collective-permute-start | bytes 56 | tf_op jit(solution)/shard_map/ppermute | solution.py:611
  223.0 350.6 %collective-permute-start.2 = (bf16[1024,2048]{1,0:T(8,128)(2,1)}, bf16[1024,2048]{1,0:T(8,128)(2,1)}, u32[]{:S(2)}, u32[]{:S(2)}) collective-permute-start(bf16[1024,2048]{1,0:T(8,128)(2,1)} %encode.2), channel_id=1, source_target_pairs={{0,8},{1,9},{2,10},{3,11},{4,12},{5,13},{6,14},{7,15},{8,0},{9,1},... | collective-permute-start | bytes 12582920 | tf_op jit(solution)/shard_map/ppermute | solution.py:613
  573.5 129.4 %collective-permute-start.3 = (bf16[384,2048]{1,0:T(8,128)(2,1)}, bf16[384,2048]{1,0:T(8,128)(2,1)}, u32[]{:S(2)}, u32[]{:S(2)}) collective-permute-start(bf16[384,2048]{1,0:T(8,128)(2,1)} %decode.2), channel_id=1, source_target_pairs={{0,8},{1,9},{2,10},{3,11},{4,12},{5,13},{6,14},{7,15},{8,0},{9,1},... | collective-permute-start | bytes 4718600 | tf_op jit(solution)/shard_map/ppermute | solution.py:617

commit v3 on v2

--- a/solution.py
+++ b/solution.py
@@ -199,7 +199,6 @@
     raws.start(0, qkv_src(0, 0))
     load_state(load, h, sums)
     settle_norm(sums, rstd, depth)
-    ring.start(0, wo_src(0))
 
     for layer in range(layers):
         last = layer + 1 == layers
@@ -225,6 +224,8 @@
                 put_blocks(big, j * (tile // LANES) + n * piece // LANES, dot(joined(xn, range(blocks)), w[:, n * piece : (n + 1) * piece]).astype(BF16))
 
         loop(n_qkv, qkv_step)
+        if layer == 0:
+            ring.start(bases[0], wo_src(0))
 
         def attention(b, at, first_head, count, filler=()):
             keep = lax.broadcasted_iota(jnp.int32, (1, span), 1) < len_ref[b + first_row // span]
@@ -251,7 +252,8 @@
         ring.wait(bases[0], wo_src(layer))
         ring.start(bases[1], w1_src(layer, 0))
         n_out = depth // piece
-        before = [slice(b * span, (b + 1) * span) for b in range(seqs - 1)]
+        half_span = span // 2
+        before = [slice(b * half_span, (b + 1) * half_span) for b in range(2 * (seqs - 1))]
         final = slice((seqs - 1) * span, seqs * span)
         attention(seqs - 1, final, 0, heads, [functools.partial(out_piece, n, at) for at in before for n in range(n_out)])
         for n in range(n_out):
@@ -392,7 +394,6 @@
     load_state(load, z, sums)
     settle_norm(sums, rstd, depth)
     raws.start(1, raw_src(0, 1))
-    ring.start(0, wo_src(0))
 
     for layer in range(layers):
         last = layer + 1 == layers
@@ -420,13 +421,20 @@
                 def _(later=later):
                     raw_ahead(later)
 
+            if layer == 0:
+                for turn in range(1, 5):
+
+                    @pl.when(j == turn)
+                    def _(turn=turn):
+                        for copy in load_enc[(turn - 1) * blocks // 4 : turn * blocks // 4]:
+                            copy.start()
+
             project(big, j * (tile // LANES), xn, slot, tile)
 
         normalize(z, rstd, xn)
+        loop(6, qkv_step)
         if layer == 0:
-            for copy in load_enc:
-                copy.start()
-        loop(6, qkv_step)
+            ring.start(bases[0], wo_src(0))
 
         if layer == 0:
             for copy in load_enc:
@@ -445,7 +453,7 @@
 
             at = pl.ds(pl.multiple_of(b * span, span), span)
             w = raw[slot].reshape(depth, tile)
-            kv_rows = min(256, kv.shape[1])
+            kv_rows = min(512, kv.shape[1])
 
             def kv_piece(n, m):
                 part = slice(m * kv_rows, (m + 1) * kv_rows)

time: 713 us -> 703 us (0.986)
  Pallas kernels: 689 us -> 679 us
    pallas_call x2, Pallas kernels: 259 us -> 250 us  [decoder_call(): pl.pallas_call(functools.partial(decoder_kernel, first_seq * span, out_se...]
  transfers between devices with their start and end apart: 4 -> 4, of which waited for: 0 -> 0; matrix products, arithmetic and copies ran while one was open for 0% -> 0% of each run, Pallas kernels for 98% -> 97%
where the time goes in v3:
time: 703 us; the launch traced here: 697 us
  Pallas kernels  679 us (97%)
  starting transfers between devices  14.2 us (2%)
    pallas_call x2, Pallas kernels, encoder_call(): pl.pallas_call(functools.partial(encoder_kernel, first_seq * span, seqs,...  429 us
    pallas_call x2, Pallas kernels, decoder_call(): pl.pallas_call(functools.partial(decoder_kernel, first_seq * span, out_se...  250 us
  transfers between devices with their start and end apart: 4, of which 0 were waited for; matrix products, arithmetic and copies ran while one was open for 0% of the time, Pallas kernels for 97%

profile of v3, /device:TPU:28, one launch (start us, length us, event | category | flops | bytes accessed | tf_op | source)
XLA Modules:
  0.0 696.7 jit_solution(12891539095661497579)
XLA Ops:
  0.0 8.0 %collective-permute-start.1 = (bf16[4,192,2048]{2,1,0:T(8,128)(2,1)}, bf16[4,192,2048]{2,1,0:T(8,128)(2,1)}, u32[]{:S(2)}, u32[]{:S(2)}) collective-permute-start(bf16[4,192,2048]{2,1,0:T(8,128)(2,1)} %param.16), channel_id=1, source_target_pairs={{0,8},{1,9},{2,10},{3,11},{4,12},{5,13},{6,14},{7,15},{8,0},{9,1},... | collective-permute-start | bytes 9437192 | tf_op jit(solution)/shard_map/ppermute | solution.py:618
  8.0 0.0 collective-permute-start
  8.0 214.4 %encode.2 = bf16[1024,2048]{1,0:T(8,128)(2,1)} custom-call(s32[4]{0:T(128)} %len_ref.5, bf16[2048,2048]{1,0:T(8,128)(2,1)} %bitcast.17, bf16[2,2048,3,16,128]{4,3,2,1,0:T(8,128)(2,1)} %wqkv.5, bf16[2,2048,2048]{2,1,0:T(8,128)(2,1)} %bitcast.9, bf16[2,2048,6144]{2,1,0:T(8,128)(2,1)} %w1.5, bf16[2,6144,2048]{2,1,0:T(8,128)(2,1)} %w2.5), custom_call_target="tpu_custom_call" | custom-call | flops 180388626432 | bytes 167772160 | tf_op jit(solution)/shard_map/encode/pallas_call | solution.py:315
  222.4 6.0 collective-permute-start.2
  228.5 214.4 %encode.3.enc_ref = bf16[1024,2048]{1,0:T(8,128)(2,1)} custom-call(s32[4]{0:T(128)} %len_ref.5, bf16[2048,2048]{1,0:T(8,128)(2,1)} %bitcast.18, bf16[2,2048,3,16,128]{4,3,2,1,0:T(8,128)(2,1)} %wqkv.5, bf16[2,2048,2048]{2,1,0:T(8,128)(2,1)} %bitcast.10, bf16[2,2048,6144]{2,1,0:T(8,128)(2,1)} %w1.5, bf16[2,6144,2048]{2,1,0:T(8,128)(2,1)} %w2.5), custom_call_target="tpu_custom_call" | custom-call | flops 180388626432 | bytes 167772160 | tf_op jit(solution)/shard_map/encode/pallas_call | solution.py:315
  442.9 0.0 collective-permute-done.1
  442.9 125.4 %decode.2 = bf16[384,2048]{1,0:T(8,128)(2,1)} custom-call(s32[4]{0:T(128)} %len_ref.5, bf16[768,2048]{1,0:T(8,128)(2,1)} %bitcast.y_ref, bf16[1024,2048]{1,0:T(8,128)(2,1)} %encode.3.enc_ref, bf16[2,2048,3,16,128]{4,3,2,1,0:T(8,128)(2,1)} %wqkv.7, bf16[2,2048,2048]{2,1,0:T(8,128)(2,1)} %bitcast.11, bf16[2,2048,16,128]{3,2,1,0:T(8,128)(2,1)} %bitcast.13, ...), custom_call_target="tpu_custom_call" | custom-call | flops 116098334720 | bytes 234881024 | tf_op jit(solution)/shard_map/decode/pallas_call | solution.py:569
  568.3 0.1 collective-permute-start.3
  568.4 0.0 collective-permute-done.len_ref
  568.4 0.0 collective-permute-done.2.enc_ref
  568.4 125.0 %decode.3 = bf16[768,2048]{1,0:T(8,128)(2,1)} custom-call(s32[4]{0:T(128)} %collective-permute-done.len_ref, bf16[768,2048]{1,0:T(8,128)(2,1)} %bitcast.19, bf16[1024,2048]{1,0:T(8,128)(2,1)} %collective-permute-done.2.enc_ref, bf16[2,2048,3,16,128]{4,3,2,1,0:T(8,128)(2,1)} %wqkv.7, bf16[2,2048,2048]{2,1,0:T(8,128)(2,1)} %bitcast.12, ...), custom_call_target="tpu_custom_call" | custom-call | flops 116098334720 | bytes 234881024 | tf_op jit(solution)/shard_map/decode/pallas_call | solution.py:569
  693.5 0.0 collective-permute-done.3
  693.5 2.7 constant_dynamic-update-slice_fusion
Async XLA Ops:
  0.0 442.9 %collective-permute-start.1 = (bf16[4,192,2048]{2,1,0:T(8,128)(2,1)}, bf16[4,192,2048]{2,1,0:T(8,128)(2,1)}, u32[]{:S(2)}, u32[]{:S(2)}) collective-permute-start(bf16[4,192,2048]{2,1,0:T(8,128)(2,1)} %param.16), channel_id=1, source_target_pairs={{0,8},{1,9},{2,10},{3,11},{4,12},{5,13},{6,14},{7,15},{8,0},{9,1},... | collective-permute-start | bytes 9437192 | tf_op jit(solution)/shard_map/ppermute | solution.py:618
  8.0 560.4 %collective-permute-start = (s32[4]{0:T(128)}, s32[4]{0:T(128)}, u32[]{:S(2)}, u32[]{:S(2)}) collective-permute-start(s32[4]{0:T(128)} %len_ref.5), channel_id=1, source_target_pairs={{0,8},{1,9},{2,10},{3,11},{4,12},{5,13},{6,14},{7,15},{8,0},{9,1},... | collective-permute-start | bytes 56 | tf_op jit(solution)/shard_map/ppermute | solution.py:619
  222.4 346.0 %collective-permute-start.2 = (bf16[1024,2048]{1,0:T(8,128)(2,1)}, bf16[1024,2048]{1,0:T(8,128)(2,1)}, u32[]{:S(2)}, u32[]{:S(2)}) collective-permute-start(bf16[1024,2048]{1,0:T(8,128)(2,1)} %encode.2), channel_id=1, source_target_pairs={{0,8},{1,9},{2,10},{3,11},{4,12},{5,13},{6,14},{7,15},{8,0},{9,1},... | collective-permute-start | bytes 12582920 | tf_op jit(solution)/shard_map/ppermute | solution.py:621
  568.3 125.2 %collective-permute-start.3 = (bf16[384,2048]{1,0:T(8,128)(2,1)}, bf16[384,2048]{1,0:T(8,128)(2,1)}, u32[]{:S(2)}, u32[]{:S(2)}) collective-permute-start(bf16[384,2048]{1,0:T(8,128)(2,1)} %decode.2), channel_id=1, source_target_pairs={{0,8},{1,9},{2,10},{3,11},{4,12},{5,13},{6,14},{7,15},{8,0},{9,1},... | collective-permute-start | bytes 4718600 | tf_op jit(solution)/shard_map/ppermute | solution.py:625
